TPU v7x, 32 devices: a whole 2x2x4 slice. The times are simulated.
32 devices in a mesh: grp: 2 (over y), depth: 4 (over x, core), shot: 4 (over z).
Axes of the slice: x: 2, y: 2, z: 4, core: 2. Of those that a mesh axis runs over, the one named last changes fastest.
Arguments:
- forward: bfloat16 [4, 8, 32, 32, 128], P(None, ('grp', 'shot'), 'depth'), parts along dimension 1, may hold values from -6 to 6
- adjoint_last: float32 [8, 32, 32, 128], P(('grp', 'shot'), 'depth'), parts along dimension 0, may hold values from -6 to 6
- adjoint_late: float32 [8, 32, 32, 128], P(('grp', 'shot'), 'depth'), parts along dimension 0, may hold values from -6 to 6
- residuals: float32 [8, 4, 256], P(('grp', 'shot')), parts along dimension 0, may hold values from -6 to 6
- source_cells: int32 [8, 3], P('grp'), parts along dimension 0, may hold values from 0 to 127, as said below
- receiver_cells: int32 [8, 256, 3], P('grp'), parts along dimension 0, may hold values from 0 to 127, as said below
- assignment: int32 [8], P('grp'), parts along dimension 0, may hold values from 0 to 3, each once
- model: float32 [6, 32, 16, 64], P(None, ('grp', 'depth'), 'shot'), parts along dimension 1, may hold values from -0.4 to 2, as said below
Outputs:
- adjoint_first: float32 [8, 32, 32, 128], P(('grp', 'shot'), 'depth'), parts along dimension 0
- gradients: float32 [6, 32, 16, 64], P(None, ('grp', 'depth'), 'shot'), parts along dimension 1
There are 2 independent parts, one for each index of `grp`. A program takes and returns all parts, laid end to end along the dimension named above; each array names one. Nothing has to cross between parts.
Inputs may be any that keep to these rules, and one draw needn't show every extreme that they name: `source_cells`: each row holds the depth, second and third cell index of a source inside the grid of 32 x 32 x 128 cells. `receiver_cells`: each entry holds the depth, second and third cell index of a receiver inside the grid; receivers may share a cell. `assignment`: each survey row is used by exactly one shot. `model`: channel 0 (depth with depth) lies in 1 to 2; channels 1 and 2 (second with second, third with third) lie in 0.25 to 1; channels 3 to 5 (depth with second, depth with third, second with third) lie in -0.4 to 0.4.
All inputs are finite; a program needn't handle non-finite values.
Results may differ from a plain program's by a relative error of at most 0.0003.
Values sent between devices are 32-bit elements; how exact they have to be, the bound alone decides.
No kernel may reach another device: no remote copies, remote signals or barrier semaphores. Data moves between devices by JAX's collectives and lax.ppermute only.
A program may use at most 128 MiB of HBM per device.

v0:
```python
import functools

import jax
import jax.numpy as jnp
from jax import lax
from jax.experimental import pallas as pl
from jax.experimental.pallas import tpu as pltpu
from jax.sharding import PartitionSpec as P

MUTE = 3
TIME_SQUARED = 0.2
PAD = 8
VMEM = pl.BlockSpec(memory_space=pltpu.VMEM)
SMEM = pl.BlockSpec(memory_space=pltpu.SMEM)
HBM = pl.BlockSpec(memory_space=pltpu.HBM)
LIMIT = pltpu.CompilerParams(vmem_limit_bytes=16 * 1024 * 1024)


def refine_matrix(coarse):
    row = lax.broadcasted_iota(jnp.int32, (coarse, 2 * coarse), 0)
    column = lax.broadcasted_iota(jnp.int32, (coarse, 2 * coarse), 1)
    here = column // 2
    after = jnp.minimum(here + 1, coarse - 1)
    odd = (column % 2) == 1
    at_here = jnp.where(row == here, 1.0, 0.0)
    at_after = jnp.where(row == after, 1.0, 0.0)
    return jnp.where(odd, 0.5 * (at_here + at_after), at_here).astype(jnp.float32)


def exact_dot(left, right, contract=((1,), (0,))):
    right = right.astype(jnp.bfloat16)
    total = None
    for _ in range(3):
        part = left.astype(jnp.bfloat16)
        left = left - part.astype(jnp.float32)
        product = lax.dot_general(
            part, right, (contract, ((), ())), preferred_element_type=jnp.float32
        )
        total = product if total is None else total + product
    return total


def even_depth():
    return lax.axis_index("depth") % 2 == 0


def pack_model(model_ref, own_ref, first_ref, second_ref, *, reach):
    channels, coarse_len, share, coarse_columns = model_ref.shape
    half = channels // 2
    for z in range(coarse_len):
        for k in range(half):
            at = (z * half + k) * share
            own_ref[at : at + share, 0:coarse_columns] = model_ref[k, z]
            own_ref[at : at + share, coarse_columns:] = model_ref[k + half, z]
    part = reach * half * share
    total = coarse_len * half * share
    even = even_depth()

    @pl.when(even)
    def _():
        first_ref[...] = own_ref[total - part : total, :]
        second_ref[...] = own_ref[0:part, :]

    @pl.when(jnp.logical_not(even))
    def _():
        first_ref[...] = own_ref[0:part, :]
        second_ref[...] = own_ref[total - part : total, :]


def pack_fields(
    current_ref, previous_ref, forward_ref, field_first, field_second, weights, sems, *, steps
):
    depth_len = current_ref.shape[1]
    up, down = steps + 1, steps

    def fill(bottom, top):
        copies = [
            pltpu.make_async_copy(forward_ref.at[:, 0, depth_len - 1], weights, sems.at[0]),
            pltpu.make_async_copy(
                current_ref.at[0, depth_len - up : depth_len], bottom.at[0:up], sems.at[1]
            ),
            pltpu.make_async_copy(
                previous_ref.at[0, depth_len - up + 1 : depth_len],
                bottom.at[up : 2 * up - 1],
                sems.at[2],
            ),
            pltpu.make_async_copy(current_ref.at[0, 0:down], top.at[0:down], sems.at[3]),
            pltpu.make_async_copy(
                previous_ref.at[0, 0 : down - 1], top.at[down : 2 * down - 1], sems.at[4]
            ),
        ]
        for copy in copies:
            copy.start()
        copies[0].wait()
        for i in range(steps):
            bottom[2 * up - 1 + i] = weights[i].astype(jnp.float32)
        for copy in copies[1:]:
            copy.wait()

    even = even_depth()

    @pl.when(even)
    def _():
        fill(field_first, field_second)

    @pl.when(jnp.logical_not(even))
    def _():
        fill(field_second, field_first)


def join_model(own_ref, first_ref, second_ref, out_ref, *, layer, depth_count):
    part = first_ref.shape[0]
    own = own_ref.shape[0]
    out_ref[part : part + own, :] = own_ref[...]
    even = even_depth()
    last = lax.axis_index("depth") == depth_count - 1

    @pl.when(even)
    def _():
        out_ref[0:part, :] = second_ref[...]
        out_ref[part + own : 2 * part + own, :] = first_ref[...]

    @pl.when(jnp.logical_not(even))
    def _():
        out_ref[0:part, :] = first_ref[...]
        out_ref[part + own : 2 * part + own, :] = second_ref[...]

    @pl.when(last)
    def _():
        out_ref[part + own : part + own + layer, :] = own_ref[own - layer : own, :]


def injection(assign_ref, residual_ref, receiver_ref, out_ref, *, steps, depth_len, rows):
    receivers = receiver_ref.shape[2]
    columns = out_ref.shape[3]
    count = out_ref.shape[1]
    geometry = assign_ref[lax.axis_index("shot")]
    first = lax.axis_index("depth") * depth_len - steps
    depth = receiver_ref[0, pl.ds(geometry, 1), :] - first
    flat = depth * rows + receiver_ref[1, pl.ds(geometry, 1), :]
    flat = jnp.where((depth >= 0) & (depth < count), flat, -1)
    cells = lax.broadcasted_iota(jnp.int32, (count * rows, receivers), 0)
    one_hot = jnp.where(cells == flat, 1.0, 0.0).astype(jnp.bfloat16)
    lanes = lax.broadcasted_iota(jnp.int32, (columns, receivers), 0)
    here = lanes == receiver_ref[2, pl.ds(geometry, 1), :]
    for i in range(steps):
        left = residual_ref[0, i : i + 1, :]
        total = None
        for _ in range(3):
            rounded = left.astype(jnp.bfloat16).astype(jnp.float32)
            left = left - rounded
            values = jnp.where(here, rounded, 0.0).astype(jnp.bfloat16)
            product = lax.dot_general(
                one_hot, values, (((1,), (1,)), ((), ())), preferred_element_type=jnp.float32
            )
            total = product if total is None else total + product
        out_ref[i] = total.reshape(count, rows, columns)


def slopes_at(field, across, bend, e, rows):
    inner = slice(PAD, PAD + rows)
    before = slice(PAD - 1, PAD - 1 + rows)
    after = slice(PAD + 1, PAD + 1 + rows)
    twice = 2.0 * field[e, inner, :]
    slopes = [
        field[e + 1, inner, :] - twice + field[e - 1, inner, :],
        field[e, after, :] - twice + field[e, before, :],
        bend[e],
        (field[e + 1, after, :] - field[e + 1, before, :])
        - (field[e - 1, after, :] - field[e - 1, before, :]),
        across[e + 1, inner, :] - across[e - 1, inner, :],
        across[e, after, :] - across[e, before, :],
    ]
    return twice, slopes


def columns_of(field, across, bend, lowest, highest, rows):
    columns = field.shape[2]
    inner = slice(PAD, PAD + rows)
    lane = lax.broadcasted_iota(jnp.int32, (rows, columns), 1)
    for e in range(lowest, highest + 1):
        value = field[e, inner, :]
        right = jnp.where(lane == columns - 1, 0.0, pltpu.roll(value, columns - 1, 1))
        left = jnp.where(lane == 0, 0.0, pltpu.roll(value, 1, 1))
        across[e, inner, :] = right - left
        bend[e] = right + left - 2.0 * value


def clear_rim(field, rows):
    height, _, columns = field.shape
    rim = jnp.zeros((height, PAD, columns), jnp.float32)
    field[:, 0:PAD, :] = rim
    field[:, PAD + rows : 2 * PAD + rows, :] = rim


def prepare(
    current_ref,
    previous_ref,
    forward_ref,
    first_ref,
    second_ref,
    added_ref,
    field,
    start_slopes,
    start_base,
    start_totals,
    weights,
    across,
    bend,
    older,
    *,
    steps,
    depth_count,
):
    depth_len, rows, _ = current_ref.shape[1:]
    up, down = steps + 1, steps
    height = up + depth_len + down
    depth_index = lax.axis_index("depth")
    is_even = depth_index % 2 == 0
    inner = slice(PAD, PAD + rows)
    clear_rim(field, rows)
    clear_rim(across, rows)
    field[up : up + depth_len, inner, :] = current_ref[0]
    older[up : up + depth_len] = previous_ref[0]
    for i in range(steps):
        weights[i, 1 : depth_len + 1] = forward_ref[i, 0].astype(jnp.float32)

    def from_above(ref):
        field[0:up, inner, :] = ref[0:up]
        older[1:up] = ref[up : 2 * up - 1]
        for i in range(steps):
            weights[i, 0] = ref[2 * up - 1 + i]

    def from_below(ref):
        field[up + depth_len : height, inner, :] = ref[0:down]
        older[up + depth_len : height - 1] = ref[down : 2 * down - 1]

    @pl.when(is_even)
    def _():
        from_above(second_ref)
        from_below(first_ref)

    @pl.when(jnp.logical_not(is_even))
    def _():
        from_above(first_ref)
        from_below(second_ref)

    @pl.when(depth_index == 0)
    def _():
        field[0:up, inner, :] = jnp.zeros((up,) + current_ref.shape[2:], jnp.float32)
        older[0:up] = jnp.zeros((up,) + current_ref.shape[2:], jnp.float32)

    @pl.when(depth_index == depth_count - 1)
    def _():
        field[up + depth_len : height, inner, :] = jnp.zeros(
            (down,) + current_ref.shape[2:], jnp.float32
        )
        older[up + depth_len : height] = jnp.zeros((down,) + current_ref.shape[2:], jnp.float32)

    columns_of(field, across, bend, 0, height - 1, rows)
    for e in range(1, height - 1):
        twice, slopes = slopes_at(field, across, bend, e, rows)
        for k, slope in enumerate(slopes):
            start_slopes[k, e - 1] = slope
            if up - 1 <= e < up + depth_len:
                start_totals[k, e - up + 1] = weights[0, e - up + 1] * slope
        start_base[e - 1] = twice - older[e] + added_ref[0, e - 1]


def march(
    assign_ref,
    source_ref,
    field,
    start_slopes,
    start_base,
    start_totals,
    weights,
    added_ref,
    *refs,
    steps,
    shots,
    depth_count,
    reach,
):
    gathered = refs[:shots]
    final_ref = refs[shots]
    chunks = refs[shots + 1 : 2 * shots + 1]
    blocks, packed, coarse, even_rows, odd_rows, ones, twos, across, bend, totals, result = refs[
        2 * shots + 1 :
    ]
    depth_len, rows, columns = final_ref.shape[1:]
    channels = start_slopes.shape[0]
    up, down = steps + 1, steps
    height = up + depth_len + down
    depth_index = lax.axis_index("depth")
    shot_index = lax.axis_index("shot")
    is_top = depth_index == 0
    is_last = depth_index == depth_count - 1
    coarse_rows = rows // 2
    share = coarse_rows // shots
    layers = depth_len // 2 + 2 * reach
    inner = slice(PAD, PAD + rows)
    for scratch in (ones, twos, across):
        clear_rim(scratch, rows)

    half = channels // 2
    refine = refine_matrix(columns // 2)
    none = jnp.zeros_like(refine)
    refine_pair = jnp.concatenate(
        [jnp.concatenate([refine, none], axis=1), jnp.concatenate([none, refine], axis=1)], axis=0
    )
    for j in range(shots):
        wide = exact_dot(gathered[j][...], refine_pair)
        start = (shot_index ^ j) * share
        for z in range(layers):
            for k in range(half):
                at = (z * half + k) * share
                for side in range(2):
                    coarse[z, k + side * half, pl.ds(start, share), :] = wide[
                        at : at + share, side * columns : (side + 1) * columns
                    ]
    for z in range(layers):
        for k in range(channels):
            coarse[z, k, coarse_rows : coarse_rows + 1, :] = coarse[
                z, k, coarse_rows - 1 : coarse_rows, :
            ]
            scale = TIME_SQUARED if k < 3 else 0.25 * TIME_SQUARED
            here = coarse[z, k, 0:coarse_rows, :]
            after = coarse[z, k, 1 : coarse_rows + 1, :]
            even_rows[z, k, pl.ds(0, coarse_rows, stride=2), :] = here * scale
            even_rows[z, k, pl.ds(1, coarse_rows, stride=2), :] = (here + after) * (0.5 * scale)
    for z in range(layers - 1):
        for k in range(channels):
            odd_rows[z, k] = (even_rows[z, k] + even_rows[z + 1, k]) * 0.5

    for i in range(steps):
        now = field if i == 0 else (ones if i % 2 else twos)
        old = field if i == 1 else (twos if i % 2 else ones)
        new = twos if i % 2 else ones
        if i > 0:
            columns_of(now, across, bend, i, height - 1 - i, rows)
        for e in range(i + 1, height - 1 - i):
            counted = up - 1 <= e < up + depth_len and i > 0
            stepped = i < steps - 1 or up <= e < up + depth_len
            if not (counted or stepped):
                continue
            if i == 0:
                slopes = [start_slopes[k, e - 1] for k in range(channels)]
                base = start_base[e - 1]
            else:
                twice, slopes = slopes_at(now, across, bend, e, rows)
            if counted:
                weight = weights[i, e - up + 1]
                for k in range(channels):
                    so_far = start_totals if i == 1 else totals
                    totals[k, e - up + 1] = so_far[k, e - up + 1] + weight * slopes[k]
            if stepped:
                if i > 0:
                    base = twice - old[e, inner, :] + added_ref[i, e - 1]
                z = e - up + 2 * reach
                table = even_rows if z % 2 == 0 else odd_rows
                change = table[z // 2, 0] * slopes[0]
                for k in range(1, channels):
                    change = change + table[z // 2, k] * slopes[k]
                updated = base + change
                if e < up:
                    updated = jnp.where(is_top, 0.0, updated)
                if e >= up + depth_len:
                    updated = jnp.where(is_last, 0.0, updated)
                if i < steps - 1:
                    new[e, inner, :] = updated
                else:
                    final_ref[0, e - up] = updated
    if steps == 1:
        totals[...] = start_totals[...]

    geometry = assign_ref[shot_index]
    first = depth_index * depth_len
    row = lax.broadcasted_iota(jnp.int32, (rows, columns), 0)
    lane = lax.broadcasted_iota(jnp.int32, (rows, columns), 1)
    near = (jnp.abs(row - source_ref[geometry, 1]) <= MUTE) & (
        jnp.abs(lane - source_ref[geometry, 2]) <= MUTE
    )
    near = jnp.where(near, 1, 0)
    masks = []
    for e in range(depth_len + 1):
        close = jnp.abs(first + e - 1 - source_ref[geometry, 0]) <= MUTE
        masks.append(near * jnp.where(close, 1, 0) > 0)
    rim_scale = jnp.where(is_top, 0.0, 0.5)
    last_scale = jnp.where(is_last, 1.0, 0.5)
    depth_half = depth_len // 2
    line = lax.broadcasted_iota(jnp.int32, (coarse_rows, columns), 0)
    for k in range(channels):
        kept = [jnp.where(masks[e], 0.0, totals[k, e]) for e in range(depth_len + 1)]
        for z in range(depth_half):
            above = kept[0] * rim_scale if z == 0 else kept[2 * z] * 0.5
            below = kept[2 * z + 2] * (last_scale if z == depth_half - 1 else 0.5)
            slot = (k * depth_half + z) % result.shape[0]
            result[slot] = kept[2 * z + 1] + above + below
            even = result[slot, pl.ds(0, coarse_rows, stride=2), :]
            odd = 0.5 * result[slot, pl.ds(1, coarse_rows, stride=2), :]
            ones[slot, PAD : PAD + coarse_rows, :] = odd
            tail = jnp.where(line == coarse_rows - 1, odd, 0.0)
            value = even + odd + ones[slot, PAD - 1 : PAD - 1 + coarse_rows, :] + tail
            at = (k * depth_half + z) * coarse_rows
            blocks[at : at + coarse_rows, :] = value
    rows_half = half * depth_half * coarse_rows
    gather_rows = lambda low: jnp.concatenate([refine, none] if low else [none, 0.25 * refine], axis=0)
    packed[...] = exact_dot(blocks[0:rows_half, :], gather_rows(True), ((1,), (1,))) + exact_dot(
        blocks[rows_half : 2 * rows_half, :], gather_rows(False), ((1,), (1,))
    )
    for j in range(shots):
        start = (shot_index ^ j) * share
        for layer in range(half * depth_half):
            chunks[j][layer * share : (layer + 1) * share, :] = packed[
                pl.ds(layer * coarse_rows + start, share), :
            ]


def finish(*refs, steps):
    parts, out_ref = refs[:-1], refs[-1]
    channels, depth_len, share, columns = out_ref.shape
    total = parts[0][...]
    for part in parts[1:]:
        total = total + part[...]
    total = total / steps
    half = channels // 2
    for k in range(half):
        for z in range(depth_len):
            at = (k * depth_len + z) * share
            out_ref[k, z] = total[at : at + share, 0:columns]
            out_ref[k + half, z] = total[at : at + share, columns:]


def local_part(
    forward, adjoint_last, adjoint_late, residuals, source_cells, receiver_cells, assignment, model
):
    steps = forward.shape[0]
    shots_here, depth_len, rows, columns = adjoint_last.shape
    channels, coarse_len, share, coarse_columns = model.shape
    shots = lax.axis_size("shot")
    depth_count = lax.axis_size("depth")
    reach = (steps + 1) // 2
    assert shots_here == 1 and depth_count % 2 == 0 and shots & (shots - 1) == 0
    assert channels == 6 and 2 * coarse_columns == columns
    assert depth_len > steps and coarse_len >= reach and share * shots * 2 == rows
    f32 = jnp.float32
    shape = lambda *dims: jax.ShapeDtypeStruct(dims, f32)
    local = lambda *dims: pltpu.VMEM(dims, f32)
    near = lambda array: pltpu.with_memory_space_constraint(array, pltpu.VMEM)
    far = lambda array: pltpu.with_memory_space_constraint(array, pltpu.HBM)
    first_pairs = [(i, i ^ 1) for i in range(depth_count)]
    second_pairs = [(i, (i + 1 if i % 2 else i - 1) % depth_count) for i in range(depth_count)]

    def moved(array, axis, pairs):
        return near(lax.ppermute(array, axis, pairs))

    half = channels // 2
    part = reach * half * share
    own_rows = coarse_len * half * share
    halo = 3 * steps + 1
    own, model_first, model_second = pl.pallas_call(
        functools.partial(pack_model, reach=reach),
        in_specs=[VMEM],
        out_specs=[VMEM] * 3,
        out_shape=[local(own_rows, columns), local(part, columns), local(part, columns)],
        name="pack_model",
        compiler_params=LIMIT,
    )(far(model))
    model_second = moved(model_second, "depth", second_pairs)
    model_first = moved(model_first, "depth", first_pairs)
    field_first, field_second = pl.pallas_call(
        functools.partial(pack_fields, steps=steps),
        in_specs=[HBM] * 3,
        out_specs=[VMEM] * 2,
        out_shape=[local(halo, rows, columns)] * 2,
        scratch_shapes=[
            pltpu.VMEM((steps, rows, columns), jnp.bfloat16),
            pltpu.SemaphoreType.DMA((5,)),
        ],
        name="pack_fields",
        compiler_params=LIMIT,
    )(far(adjoint_last), far(adjoint_late), far(forward))
    field_second = moved(field_second, "depth", second_pairs)
    field_first = moved(field_first, "depth", first_pairs)
    height = depth_len + 2 * steps + 1
    added = pl.pallas_call(
        functools.partial(injection, steps=steps, depth_len=depth_len, rows=rows),
        in_specs=[SMEM, VMEM, VMEM],
        out_specs=VMEM,
        out_shape=local(steps, height - 2, rows, columns),
        name="injection",
        compiler_params=LIMIT,
    )(far(assignment), far(residuals), far(receiver_cells.transpose(2, 0, 1)))
    joined_rows = own_rows + 2 * part
    joined = pl.pallas_call(
        functools.partial(join_model, layer=half * share, depth_count=depth_count),
        in_specs=[VMEM] * 3,
        out_specs=VMEM,
        out_shape=local(joined_rows, columns),
        name="join_model",
        compiler_params=LIMIT,
    )(near(own), model_first, model_second)
    swap = lambda array, j: moved(array, "shot", [(i, i ^ j) for i in range(shots)])
    gathered = [near(joined)] + [swap(joined, j) for j in range(1, shots)]
    padded = rows + 2 * PAD
    prepared = pl.pallas_call(
        functools.partial(prepare, steps=steps, depth_count=depth_count),
        in_specs=[VMEM] * 6,
        out_specs=[VMEM] * 5,
        out_shape=[
            local(height, padded, columns),
            local(channels, height - 2, rows, columns),
            local(height - 2, rows, columns),
            local(channels, depth_len + 1, rows, columns),
            local(steps, depth_len + 1, rows, columns),
        ],
        scratch_shapes=[
            pltpu.VMEM((height, padded, columns), f32),
            pltpu.VMEM((height, rows, columns), f32),
            pltpu.VMEM((height, rows, columns), f32),
        ],
        name="prepare",
        compiler_params=LIMIT,
    )(adjoint_last, adjoint_late, forward, field_first, field_second, near(added))
    layers = coarse_len + 2 * reach
    chunk = local(half * coarse_len * share, columns)
    final, *chunks = pl.pallas_call(
        functools.partial(march, steps=steps, shots=shots, depth_count=depth_count, reach=reach),
        in_specs=[SMEM, SMEM] + [VMEM] * (6 + shots),
        out_specs=[VMEM] * (1 + shots),
        out_shape=[shape(1, depth_len, rows, columns)] + [chunk] * shots,
        scratch_shapes=[
            pltpu.VMEM((channels * coarse_len * rows // 2, columns), f32),
            pltpu.VMEM((half * coarse_len * rows // 2, columns), f32),
            pltpu.VMEM((layers, channels, rows // 2 + PAD, columns), f32),
            pltpu.VMEM((layers, channels, rows, columns), f32),
            pltpu.VMEM((layers - 1, channels, rows, columns), f32),
            pltpu.VMEM((height, padded, columns), f32),
            pltpu.VMEM((height, padded, columns), f32),
            pltpu.VMEM((height, padded, columns), f32),
            pltpu.VMEM((height, rows, columns), f32),
            pltpu.VMEM((channels, depth_len + 1, rows, columns), f32),
            pltpu.VMEM((4, rows, columns), f32),
        ],
        name="march",
        compiler_params=LIMIT,
    )(
        far(assignment),
        far(source_cells),
        *map(near, prepared),
        near(added),
        *gathered,
    )
    parts = [near(chunks[0])] + [swap(chunks[j], j) for j in range(1, shots)]
    gradients = pl.pallas_call(
        functools.partial(finish, steps=steps),
        in_specs=[VMEM] * shots,
        out_specs=VMEM,
        out_shape=shape(*model.shape),
        name="finish",
        compiler_params=LIMIT,
    )(*parts)
    return final, gradients


def solution(mesh):
    placed = (
        P(None, ("grp", "shot"), "depth", None, None),
        P(("grp", "shot"), "depth", None, None),
        P(("grp", "shot"), "depth", None, None),
        P(("grp", "shot"), None, None),
        P("grp", None),
        P("grp", None, None),
        P("grp"),
        P(None, ("grp", "depth"), "shot", None),
    )
    return jax.shard_map(
        local_part,
        mesh=mesh,
        in_specs=placed,
        out_specs=(
            P(("grp", "shot"), "depth", None, None),
            P(None, ("grp", "depth"), "shot", None),
        ),
        check_vma=False,
    )
```

profile of v0, /device:TPU:0, one launch (start us, length us, event | category | flops | bytes accessed | tf_op | source)
XLA Modules:
  0.0 32.1 jit_solution(15375569664582346269)
XLA Ops:
  0.6 0.0 copy-start.1
  0.6 0.0 copy-start.2
  0.6 0.0 copy-start
  0.7 1.1 %pack_fields.1 = (f32[13,32,128]{2,1,0:T(8,128)S(1)}, f32[13,32,128]{2,1,0:T(8,128)S(1)}) custom-call(f32[1,8,32,128]{3,2,1,0:T(8,128)} %current_ref.3, f32[1,8,32,128]{3,2,1,0:T(8,128)} %previous_ref.3, bf16[4,1,8,32,128]{4,3,2,1,0:T(8,128)(2,1)} %forward_ref.3), custom_call_target="tpu_custom_call" | custom-call | tf_op jit(solution)/shard_map/pack_fields/pallas_call | solution.py:472
  1.7 0.6 %collective-permute-start = (f32[13,32,128]{2,1,0:T(8,128)S(1)}, f32[13,32,128]{2,1,0:T(8,128)S(1)}, u32[]{:S(2)}, u32[]{:S(2)}) collective-permute-start(f32[13,32,128]{2,1,0:T(8,128)S(1)} %get-tuple-element.17), channel_id=1, source_target_pairs={{0,4},{4,0},{8,12},{12,8},{1,5},{5,1},{9,13},{13,9},{2,6},{6,2},{1... | collective-permute-start | bytes 638984 | tf_op jit(solution)/shard_map/ppermute | solution.py:456
  2.3 2.6 %collective-permute-start.1 = (f32[13,32,128]{2,1,0:T(8,128)S(1)}, f32[13,32,128]{2,1,0:T(8,128)S(1)}, u32[]{:S(2)}, u32[]{:S(2)}) collective-permute-start(f32[13,32,128]{2,1,0:T(8,128)S(1)} %get-tuple-element.18), channel_id=1, source_target_pairs={{0,12},{4,8},{8,4},{12,0},{1,13},{5,9},{9,5},{13,1},{2,14},{6,10},... | collective-permute-start | bytes 638984 | tf_op jit(solution)/shard_map/ppermute | solution.py:456
  4.9 0.9 %pack_model.1 = (f32[48,128]{1,0:T(8,128)S(1)}, f32[24,128]{1,0:T(8,128)S(1)}, f32[24,128]{1,0:T(8,128)S(1)}) custom-call(f32[6,4,4,64]{3,2,1,0:T(4,128)} %model_ref.1), custom_call_target="tpu_custom_call" | custom-call | tf_op jit(solution)/shard_map/pack_model/pallas_call | solution.py:462
  5.8 0.1 collective-permute-start.2
  5.9 0.0 collective-permute-start.3
  5.9 1.1 %collective-permute-done.2.first_ref = f32[24,128]{1,0:T(8,128)S(1)} collective-permute-done((f32[24,128]{1,0:T(8,128)S(1)}, f32[24,128]{1,0:T(8,128)S(1)}, u32[]{:S(2)}, u32[]{:S(2)}) %collective-permute-start.2) | collective-permute-done | bytes 12320 | tf_op jit(solution)/shard_map/ppermute | solution.py:456
  7.0 3.7 %collective-permute-done.3.second_ref = f32[24,128]{1,0:T(8,128)S(1)} collective-permute-done((f32[24,128]{1,0:T(8,128)S(1)}, f32[24,128]{1,0:T(8,128)S(1)}, u32[]{:S(2)}, u32[]{:S(2)}) %collective-permute-start.3) | collective-permute-done | bytes 12320 | tf_op jit(solution)/shard_map/ppermute | solution.py:456
  10.7 1.4 %collective-permute-start.4 = (f32[96,128]{1,0:T(8,128)S(1)}, f32[96,128]{1,0:T(8,128)S(1)}, u32[]{:S(2)}, u32[]{:S(2)}) collective-permute-start(f32[96,128]{1,0:T(8,128)S(1)} %join_model.1.refs_0_), channel_id=1, source_target_pairs={{0,1},{1,0},{2,3},{3,2},{4,5},{5,4},{6,7},{7,6},{8,9},{9,8},{10,11... | collective-permute-start | bytes 147464 | tf_op jit(solution)/shard_map/ppermute | solution.py:456
  12.1 2.6 %collective-permute-start.5 = (f32[96,128]{1,0:T(8,128)S(1)}, f32[96,128]{1,0:T(8,128)S(1)}, u32[]{:S(2)}, u32[]{:S(2)}) collective-permute-start(f32[96,128]{1,0:T(8,128)S(1)} %join_model.1.refs_0_), channel_id=1, source_target_pairs={{0,2},{1,3},{2,0},{3,1},{4,6},{5,7},{6,4},{7,5},{8,10},{9,11},{10,... | collective-permute-start | bytes 147464 | tf_op jit(solution)/shard_map/ppermute | solution.py:456
  14.7 0.4 %collective-permute-start.6 = (f32[96,128]{1,0:T(8,128)S(1)}, f32[96,128]{1,0:T(8,128)S(1)}, u32[]{:S(2)}, u32[]{:S(2)}) collective-permute-start(f32[96,128]{1,0:T(8,128)S(1)} %join_model.1.refs_0_), channel_id=1, source_target_pairs={{0,3},{1,2},{2,1},{3,0},{4,7},{5,6},{6,5},{7,4},{8,11},{9,10},{10,... | collective-permute-start | bytes 147464 | tf_op jit(solution)/shard_map/ppermute | solution.py:456
  15.1 1.7 %injection.1.added_ref = f32[4,15,32,128]{3,2,1,0:T(8,128)S(1)} custom-call(s32[4]{0:T(128)} %assign_ref.3, f32[1,4,256]{2,1,0:T(4,128)} %residual_ref.1, s32[3,4,256]{2,1,0:T(4,128)} %bitcast.1), custom_call_target="tpu_custom_call" | custom-call | tf_op jit(solution)/shard_map/injection/pallas_call | solution.py:487
  16.7 0.0 collective-permute-done.first_ref
  16.8 0.0 collective-permute-done.1.second_ref
  16.8 0.0 copy-done.1
  16.8 0.0 copy-done.2
  16.8 0.0 copy-done
  16.8 0.5 %prepare.1 = (f32[17,48,128]{2,1,0:T(8,128)S(1)}, f32[6,15,32,128]{3,2,1,0:T(8,128)S(1)}, f32[15,32,128]{2,1,0:T(8,128)S(1)}, f32[6,9,32,128]{3,2,1,0:T(8,128)S(1)}, f32[4,9,32,128]{3,2,1,0:T(8,128)S(1)}) custom-call(f32[1,8,32,128]{3,2,1,0:T(8,128)S(1)} %copy-done.1, f32[1,8,32,128]{3,2,1,0:T(8,128)S(1)} %copy-done.2, ...), custom_call_target="tpu_custom_call" | custom-call | tf_op jit(solution)/shard_map/prepare/pallas_call | solution.py:507
  17.3 0.0 collective-permute-done.4.refs_1_
  17.3 1.0 %collective-permute-done.5.refs_2_ = f32[96,128]{1,0:T(8,128)S(1)} collective-permute-done((f32[96,128]{1,0:T(8,128)S(1)}, f32[96,128]{1,0:T(8,128)S(1)}, u32[]{:S(2)}, u32[]{:S(2)}) %collective-permute-start.5) | collective-permute-done | bytes 49184 | tf_op jit(solution)/shard_map/ppermute | solution.py:456
  18.2 2.4 %collective-permute-done.6.refs_3_ = f32[96,128]{1,0:T(8,128)S(1)} collective-permute-done((f32[96,128]{1,0:T(8,128)S(1)}, f32[96,128]{1,0:T(8,128)S(1)}, u32[]{:S(2)}, u32[]{:S(2)}) %collective-permute-start.6) | collective-permute-done | bytes 49184 | tf_op jit(solution)/shard_map/ppermute | solution.py:456
  20.6 3.2 %march.1 = (f32[1,8,32,128]{3,2,1,0:T(8,128)}, f32[48,128]{1,0:T(8,128)S(1)}, f32[48,128]{1,0:T(8,128)S(1)}, f32[48,128]{1,0:T(8,128)S(1)}, f32[48,128]{1,0:T(8,128)S(1)}) custom-call(s32[4]{0:T(128)} %assign_ref.3, s32[4,3]{1,0:T(4,128)} %source_ref.1, f32[17,48,128]{2,1,0:T(8,128)S(1)} %get-tuple-element.19.field, ...), custom_call_target="tpu_custom_call" | custom-call | tf_op jit(solution)/shard_map/march/pallas_call | solution.py:528
  23.8 0.0 collective-permute-start.7
  23.8 1.9 %collective-permute-start.8 = (f32[48,128]{1,0:T(8,128)S(1)}, f32[48,128]{1,0:T(8,128)S(1)}, u32[]{:S(2)}, u32[]{:S(2)}) collective-permute-start(f32[48,128]{1,0:T(8,128)S(1)} %get-tuple-element.30), channel_id=1, source_target_pairs={{0,2},{1,3},{2,0},{3,1},{4,6},{5,7},{6,4},{7,5},{8,10},{9,11},{10,... | collective-permute-start | bytes 73736 | tf_op jit(solution)/shard_map/ppermute | solution.py:456
  25.7 2.5 %collective-permute-start.9 = (f32[48,128]{1,0:T(8,128)S(1)}, f32[48,128]{1,0:T(8,128)S(1)}, u32[]{:S(2)}, u32[]{:S(2)}) collective-permute-start(f32[48,128]{1,0:T(8,128)S(1)} %get-tuple-element.31), channel_id=1, source_target_pairs={{0,3},{1,2},{2,1},{3,0},{4,7},{5,6},{6,5},{7,4},{8,11},{9,10},{10,... | collective-permute-start | bytes 73736 | tf_op jit(solution)/shard_map/ppermute | solution.py:456
  28.2 0.0 collective-permute-done.7.refs_1_
  28.2 0.4 %collective-permute-done.8.refs_2_ = f32[48,128]{1,0:T(8,128)S(1)} collective-permute-done((f32[48,128]{1,0:T(8,128)S(1)}, f32[48,128]{1,0:T(8,128)S(1)}, u32[]{:S(2)}, u32[]{:S(2)}) %collective-permute-start.8) | collective-permute-done | bytes 24608 | tf_op jit(solution)/shard_map/ppermute | solution.py:456
  28.6 2.7 %collective-permute-done.9.refs_3_ = f32[48,128]{1,0:T(8,128)S(1)} collective-permute-done((f32[48,128]{1,0:T(8,128)S(1)}, f32[48,128]{1,0:T(8,128)S(1)}, u32[]{:S(2)}, u32[]{:S(2)}) %collective-permute-start.9) | collective-permute-done | bytes 24608 | tf_op jit(solution)/shard_map/ppermute | solution.py:456
  31.4 0.7 %finish.1 = f32[6,4,4,64]{3,2,1,0:T(4,128)} custom-call(f32[48,128]{1,0:T(8,128)S(1)} %get-tuple-element.28.refs_0_, f32[48,128]{1,0:T(8,128)S(1)} %collective-permute-done.7.refs_1_, f32[48,128]{1,0:T(8,128)S(1)} %collective-permute-done.8.refs_2_, f32[48,128]{1,0:T(8,128)S(1)} %collective-permute-done.9.refs_3_), custom_call_target="tpu_custom_call" | custom-call | tf_op jit(solution)/shard_map/finish/pallas_call | solution.py:556
  (1 shorter events, 0.0 us)
Async XLA Ops:
  0.6 16.1 %copy-start.1 = (f32[1,8,32,128]{3,2,1,0:T(8,128)S(1)}, f32[1,8,32,128]{3,2,1,0:T(8,128)}, u32[]{:S(2)}) copy-start(f32[1,8,32,128]{3,2,1,0:T(8,128)} %current_ref.3) | copy-start | bytes 393220
  0.6 16.1 %copy-start.2 = (f32[1,8,32,128]{3,2,1,0:T(8,128)S(1)}, f32[1,8,32,128]{3,2,1,0:T(8,128)}, u32[]{:S(2)}) copy-start(f32[1,8,32,128]{3,2,1,0:T(8,128)} %previous_ref.3) | copy-start | bytes 393220
  0.6 16.1 %copy-start = (bf16[4,1,8,32,128]{4,3,2,1,0:T(8,128)(2,1)S(1)}, bf16[4,1,8,32,128]{4,3,2,1,0:T(8,128)(2,1)}, u32[]{:S(2)}) copy-start(bf16[4,1,8,32,128]{4,3,2,1,0:T(8,128)(2,1)} %forward_ref.3) | copy-start | bytes 786436
  1.7 15.0 %collective-permute-start = (f32[13,32,128]{2,1,0:T(8,128)S(1)}, f32[13,32,128]{2,1,0:T(8,128)S(1)}, u32[]{:S(2)}, u32[]{:S(2)}) collective-permute-start(f32[13,32,128]{2,1,0:T(8,128)S(1)} %get-tuple-element.17), channel_id=1, source_target_pairs={{0,4},{4,0},{8,12},{12,8},{1,5},{5,1},{9,13},{13,9},{2,6},{6,2},{1... | collective-permute-start | bytes 638984 | tf_op jit(solution)/shard_map/ppermute | solution.py:456
  2.3 14.5 %collective-permute-start.1 = (f32[13,32,128]{2,1,0:T(8,128)S(1)}, f32[13,32,128]{2,1,0:T(8,128)S(1)}, u32[]{:S(2)}, u32[]{:S(2)}) collective-permute-start(f32[13,32,128]{2,1,0:T(8,128)S(1)} %get-tuple-element.18), channel_id=1, source_target_pairs={{0,12},{4,8},{8,4},{12,0},{1,13},{5,9},{9,5},{13,1},{2,14},{6,10},... | collective-permute-start | bytes 638984 | tf_op jit(solution)/shard_map/ppermute | solution.py:456
  5.8 1.2 %collective-permute-start.2 = (f32[24,128]{1,0:T(8,128)S(1)}, f32[24,128]{1,0:T(8,128)S(1)}, u32[]{:S(2)}, u32[]{:S(2)}) collective-permute-start(f32[24,128]{1,0:T(8,128)S(1)} %get-tuple-element.25), channel_id=1, source_target_pairs={{0,4},{4,0},{8,12},{12,8},{1,5},{5,1},{9,13},{13,9},{2,6},{6,2},{1... | collective-permute-start | bytes 36872 | tf_op jit(solution)/shard_map/ppermute | solution.py:456
  5.9 4.8 %collective-permute-start.3 = (f32[24,128]{1,0:T(8,128)S(1)}, f32[24,128]{1,0:T(8,128)S(1)}, u32[]{:S(2)}, u32[]{:S(2)}) collective-permute-start(f32[24,128]{1,0:T(8,128)S(1)} %get-tuple-element.26), channel_id=1, source_target_pairs={{0,12},{4,8},{8,4},{12,0},{1,13},{5,9},{9,5},{13,1},{2,14},{6,10},... | collective-permute-start | bytes 36872 | tf_op jit(solution)/shard_map/ppermute | solution.py:456
  10.7 6.6 %collective-permute-start.4 = (f32[96,128]{1,0:T(8,128)S(1)}, f32[96,128]{1,0:T(8,128)S(1)}, u32[]{:S(2)}, u32[]{:S(2)}) collective-permute-start(f32[96,128]{1,0:T(8,128)S(1)} %join_model.1.refs_0_), channel_id=1, source_target_pairs={{0,1},{1,0},{2,3},{3,2},{4,5},{5,4},{6,7},{7,6},{8,9},{9,8},{10,11... | collective-permute-start | bytes 147464 | tf_op jit(solution)/shard_map/ppermute | solution.py:456
  12.1 6.1 %collective-permute-start.5 = (f32[96,128]{1,0:T(8,128)S(1)}, f32[96,128]{1,0:T(8,128)S(1)}, u32[]{:S(2)}, u32[]{:S(2)}) collective-permute-start(f32[96,128]{1,0:T(8,128)S(1)} %join_model.1.refs_0_), channel_id=1, source_target_pairs={{0,2},{1,3},{2,0},{3,1},{4,6},{5,7},{6,4},{7,5},{8,10},{9,11},{10,... | collective-permute-start | bytes 147464 | tf_op jit(solution)/shard_map/ppermute | solution.py:456
  14.7 5.9 %collective-permute-start.6 = (f32[96,128]{1,0:T(8,128)S(1)}, f32[96,128]{1,0:T(8,128)S(1)}, u32[]{:S(2)}, u32[]{:S(2)}) collective-permute-start(f32[96,128]{1,0:T(8,128)S(1)} %join_model.1.refs_0_), channel_id=1, source_target_pairs={{0,3},{1,2},{2,1},{3,0},{4,7},{5,6},{6,5},{7,4},{8,11},{9,10},{10,... | collective-permute-start | bytes 147464 | tf_op jit(solution)/shard_map/ppermute | solution.py:456
  23.8 4.4 %collective-permute-start.7 = (f32[48,128]{1,0:T(8,128)S(1)}, f32[48,128]{1,0:T(8,128)S(1)}, u32[]{:S(2)}, u32[]{:S(2)}) collective-permute-start(f32[48,128]{1,0:T(8,128)S(1)} %get-tuple-element.29), channel_id=1, source_target_pairs={{0,1},{1,0},{2,3},{3,2},{4,5},{5,4},{6,7},{7,6},{8,9},{9,8},{10,11... | collective-permute-start | bytes 73736 | tf_op jit(solution)/shard_map/ppermute | solution.py:456
  23.8 4.8 %collective-permute-start.8 = (f32[48,128]{1,0:T(8,128)S(1)}, f32[48,128]{1,0:T(8,128)S(1)}, u32[]{:S(2)}, u32[]{:S(2)}) collective-permute-start(f32[48,128]{1,0:T(8,128)S(1)} %get-tuple-element.30), channel_id=1, source_target_pairs={{0,2},{1,3},{2,0},{3,1},{4,6},{5,7},{6,4},{7,5},{8,10},{9,11},{10,... | collective-permute-start | bytes 73736 | tf_op jit(solution)/shard_map/ppermute | solution.py:456
  25.7 5.6 %collective-permute-start.9 = (f32[48,128]{1,0:T(8,128)S(1)}, f32[48,128]{1,0:T(8,128)S(1)}, u32[]{:S(2)}, u32[]{:S(2)}) collective-permute-start(f32[48,128]{1,0:T(8,128)S(1)} %get-tuple-element.31), channel_id=1, source_target_pairs={{0,3},{1,2},{2,1},{3,0},{4,7},{5,6},{6,5},{7,4},{8,11},{9,10},{10,... | collective-permute-start | bytes 73736 | tf_op jit(solution)/shard_map/ppermute | solution.py:456
where the time goes:
time: 32.3 us; the launch traced here: 32.1 us
  starting transfers between devices  12.1 us (37%)
  waiting for transfers between devices  11.2 us (35%)
  Pallas kernels  7.98 us (25%)
  between operations  0.73 us (2%)
    ppermute x10, starting transfers between devices, moved(): return near(lax.ppermute(array, axis, pairs))  12.1 us
    ppermute x10, waiting for transfers between devices, moved(): return near(lax.ppermute(array, axis, pairs))  11.2 us
    pallas_call x1, Pallas kernels, local_part(): pl.pallas_call(functools.partial(march, steps=steps, shots=shots, depth_c...  3.22 us
    pallas_call x1, Pallas kernels, local_part(): pl.pallas_call(functools.partial(injection, steps=steps, depth_len=depth_...  1.66 us
    pallas_call x1, Pallas kernels, local_part(): pl.pallas_call(functools.partial(pack_fields, steps=steps), in_specs=[HBM...  1.05 us
    pallas_call x1, Pallas kernels, local_part(): pl.pallas_call(functools.partial(pack_model, reach=reach), in_specs=[VMEM...  0.88 us
    pallas_call x1, Pallas kernels, local_part(): pl.pallas_call(functools.partial(finish, steps=steps), in_specs=[VMEM] *...  0.7 us
  transfers between devices with their start and end apart: 10, of which 6 were waited for; matrix products, arithmetic and copies ran while one was open for 0% of the time, Pallas kernels for 9%

commit v1 on v0

--- a/solution.py
+++ b/solution.py
@@ -27,17 +27,15 @@
     return jnp.where(odd, 0.5 * (at_here + at_after), at_here).astype(jnp.float32)
 
 
-def exact_dot(left, right, contract=((1,), (0,))):
+def exact_dot(left, right):
     right = right.astype(jnp.bfloat16)
-    total = None
+    parts = []
     for _ in range(3):
-        part = left.astype(jnp.bfloat16)
-        left = left - part.astype(jnp.float32)
-        product = lax.dot_general(
-            part, right, (contract, ((), ())), preferred_element_type=jnp.float32
-        )
-        total = product if total is None else total + product
-    return total
+        parts.append(left.astype(jnp.bfloat16))
+        left = left - parts[-1].astype(jnp.float32)
+    product = functools.partial(jnp.dot, preferred_element_type=jnp.float32)
+    stacked = jnp.concatenate([right, right], axis=0)
+    return product(jnp.concatenate(parts[:2], axis=1), stacked) + product(parts[2], right)
 
 
 def even_depth():
@@ -130,7 +128,38 @@
         out_ref[part + own : part + own + layer, :] = own_ref[own - layer : own, :]
 
 
-def injection(assign_ref, residual_ref, receiver_ref, out_ref, *, steps, depth_len, rows):
+def injection(
+    assign_ref,
+    source_ref,
+    residual_ref,
+    receiver_ref,
+    current_ref,
+    previous_ref,
+    forward_ref,
+    out_ref,
+    keep_ref,
+    current_out,
+    previous_out,
+    forward_out,
+    sems,
+    *,
+    steps,
+    depth_len,
+    rows,
+    depth_count,
+):
+    loads = [
+        pltpu.make_async_copy(source, target, sems.at[n])
+        for n, (source, target) in enumerate(
+            [
+                (current_ref, current_out),
+                (previous_ref, previous_out),
+                (forward_ref, forward_out),
+            ]
+        )
+    ]
+    for load in loads:
+        load.start()
     receivers = receiver_ref.shape[2]
     columns = out_ref.shape[3]
     count = out_ref.shape[1]
@@ -156,6 +185,25 @@
             total = product if total is None else total + product
         out_ref[i] = total.reshape(count, rows, columns)
 
+    depth_index = lax.axis_index("depth")
+    row = lax.broadcasted_iota(jnp.int32, (rows, columns), 0)
+    lane = lax.broadcasted_iota(jnp.int32, (rows, columns), 1)
+    near = (jnp.abs(row - source_ref[geometry, 1]) <= MUTE) & (
+        jnp.abs(lane - source_ref[geometry, 2]) <= MUTE
+    )
+    away = jnp.where(near, 0.0, 1.0)
+    for e in range(depth_len + 1):
+        close = jnp.abs(depth_index * depth_len + e - 1 - source_ref[geometry, 0]) <= MUTE
+        if e == 0:
+            scale = jnp.where(depth_index == 0, 0.0, 0.5)
+        elif e == depth_len:
+            scale = jnp.where(depth_index == depth_count - 1, 1.0, 0.5)
+        else:
+            scale = 1.0 if e % 2 else 0.5
+        keep_ref[e] = jnp.where(close, away, 1.0) * scale
+    for load in loads:
+        load.wait()
+
 
 def slopes_at(field, across, bend, e, rows):
     inner = slice(PAD, PAD + rows)
@@ -200,6 +248,7 @@
     first_ref,
     second_ref,
     added_ref,
+    keep_ref,
     field,
     start_slopes,
     start_base,
@@ -223,13 +272,15 @@
     field[up : up + depth_len, inner, :] = current_ref[0]
     older[up : up + depth_len] = previous_ref[0]
     for i in range(steps):
-        weights[i, 1 : depth_len + 1] = forward_ref[i, 0].astype(jnp.float32)
+        weights[i, 1 : depth_len + 1] = (
+            forward_ref[i, 0].astype(jnp.float32) * keep_ref[1 : depth_len + 1]
+        )
 
     def from_above(ref):
         field[0:up, inner, :] = ref[0:up]
         older[1:up] = ref[up : 2 * up - 1]
         for i in range(steps):
-            weights[i, 0] = ref[2 * up - 1 + i]
+            weights[i, 0] = ref[2 * up - 1 + i] * keep_ref[0]
 
     def from_below(ref):
         field[up + depth_len : height, inner, :] = ref[0:down]
@@ -268,8 +319,6 @@
 
 
 def march(
-    assign_ref,
-    source_ref,
     field,
     start_slopes,
     start_base,
@@ -374,29 +423,12 @@
     if steps == 1:
         totals[...] = start_totals[...]
 
-    geometry = assign_ref[shot_index]
-    first = depth_index * depth_len
-    row = lax.broadcasted_iota(jnp.int32, (rows, columns), 0)
-    lane = lax.broadcasted_iota(jnp.int32, (rows, columns), 1)
-    near = (jnp.abs(row - source_ref[geometry, 1]) <= MUTE) & (
-        jnp.abs(lane - source_ref[geometry, 2]) <= MUTE
-    )
-    near = jnp.where(near, 1, 0)
-    masks = []
-    for e in range(depth_len + 1):
-        close = jnp.abs(first + e - 1 - source_ref[geometry, 0]) <= MUTE
-        masks.append(near * jnp.where(close, 1, 0) > 0)
-    rim_scale = jnp.where(is_top, 0.0, 0.5)
-    last_scale = jnp.where(is_last, 1.0, 0.5)
     depth_half = depth_len // 2
     line = lax.broadcasted_iota(jnp.int32, (coarse_rows, columns), 0)
     for k in range(channels):
-        kept = [jnp.where(masks[e], 0.0, totals[k, e]) for e in range(depth_len + 1)]
         for z in range(depth_half):
-            above = kept[0] * rim_scale if z == 0 else kept[2 * z] * 0.5
-            below = kept[2 * z + 2] * (last_scale if z == depth_half - 1 else 0.5)
             slot = (k * depth_half + z) % result.shape[0]
-            result[slot] = kept[2 * z + 1] + above + below
+            result[slot] = totals[k, 2 * z + 1] + totals[k, 2 * z] + totals[k, 2 * z + 2]
             even = result[slot, pl.ds(0, coarse_rows, stride=2), :]
             odd = 0.5 * result[slot, pl.ds(1, coarse_rows, stride=2), :]
             ones[slot, PAD : PAD + coarse_rows, :] = odd
@@ -405,9 +437,12 @@
             at = (k * depth_half + z) * coarse_rows
             blocks[at : at + coarse_rows, :] = value
     rows_half = half * depth_half * coarse_rows
-    gather_rows = lambda low: jnp.concatenate([refine, none] if low else [none, 0.25 * refine], axis=0)
-    packed[...] = exact_dot(blocks[0:rows_half, :], gather_rows(True), ((1,), (1,))) + exact_dot(
-        blocks[rows_half : 2 * rows_half, :], gather_rows(False), ((1,), (1,))
+    gather = refine.T
+    none = jnp.zeros_like(gather)
+    packed[...] = exact_dot(
+        blocks[0:rows_half, :], jnp.concatenate([gather, none], axis=1)
+    ) + exact_dot(
+        blocks[rows_half : 2 * rows_half, :], jnp.concatenate([none, 0.25 * gather], axis=1)
     )
     for j in range(shots):
         start = (shot_index ^ j) * share
@@ -484,14 +519,31 @@
     field_second = moved(field_second, "depth", second_pairs)
     field_first = moved(field_first, "depth", first_pairs)
     height = depth_len + 2 * steps + 1
-    added = pl.pallas_call(
-        functools.partial(injection, steps=steps, depth_len=depth_len, rows=rows),
-        in_specs=[SMEM, VMEM, VMEM],
-        out_specs=VMEM,
-        out_shape=local(steps, height - 2, rows, columns),
+    added, keep, *loaded = pl.pallas_call(
+        functools.partial(
+            injection, steps=steps, depth_len=depth_len, rows=rows, depth_count=depth_count
+        ),
+        in_specs=[SMEM, SMEM, VMEM, VMEM, HBM, HBM, HBM],
+        out_specs=[VMEM] * 5,
+        out_shape=[
+            local(steps, height - 2, rows, columns),
+            local(depth_len + 1, rows, columns),
+            local(1, depth_len, rows, columns),
+            local(1, depth_len, rows, columns),
+            pltpu.VMEM(forward.shape, forward.dtype),
+        ],
+        scratch_shapes=[pltpu.SemaphoreType.DMA((3,))],
         name="injection",
         compiler_params=LIMIT,
-    )(far(assignment), far(residuals), far(receiver_cells.transpose(2, 0, 1)))
+    )(
+        far(assignment),
+        far(source_cells),
+        far(residuals),
+        far(receiver_cells.transpose(2, 0, 1)),
+        far(adjoint_last),
+        far(adjoint_late),
+        far(forward),
+    )
     joined_rows = own_rows + 2 * part
     joined = pl.pallas_call(
         functools.partial(join_model, layer=half * share, depth_count=depth_count),
@@ -506,7 +558,7 @@
     padded = rows + 2 * PAD
     prepared = pl.pallas_call(
         functools.partial(prepare, steps=steps, depth_count=depth_count),
-        in_specs=[VMEM] * 6,
+        in_specs=[VMEM] * 7,
         out_specs=[VMEM] * 5,
         out_shape=[
             local(height, padded, columns),
@@ -522,14 +574,20 @@
         ],
         name="prepare",
         compiler_params=LIMIT,
-    )(adjoint_last, adjoint_late, forward, field_first, field_second, near(added))
+    )(
+        *map(near, loaded),
+        field_first,
+        field_second,
+        near(added),
+        near(keep),
+    )
     layers = coarse_len + 2 * reach
     chunk = local(half * coarse_len * share, columns)
     final, *chunks = pl.pallas_call(
         functools.partial(march, steps=steps, shots=shots, depth_count=depth_count, reach=reach),
-        in_specs=[SMEM, SMEM] + [VMEM] * (6 + shots),
+        in_specs=[VMEM] * (6 + shots),
         out_specs=[VMEM] * (1 + shots),
-        out_shape=[shape(1, depth_len, rows, columns)] + [chunk] * shots,
+        out_shape=[local(1, depth_len, rows, columns)] + [chunk] * shots,
         scratch_shapes=[
             pltpu.VMEM((channels * coarse_len * rows // 2, columns), f32),
             pltpu.VMEM((half * coarse_len * rows // 2, columns), f32),
@@ -546,8 +604,6 @@
         name="march",
         compiler_params=LIMIT,
     )(
-        far(assignment),
-        far(source_cells),
         *map(near, prepared),
         near(added),
         *gathered,

time: 32.3 us -> 31.1 us (0.963)
  Pallas kernels: 7.98 us -> 6.91 us
  waiting for transfers between devices: 11.2 us -> 10.4 us
  local copies, waits for them, and re-layouts: 0.01 us -> 0.65 us
    pallas_call x1, Pallas kernels: 3.22 us -> 1.99 us  [local_part(): pl.pallas_call(functools.partial(march, steps=steps, shots=shots, depth_c...]
    ppermute x10, waiting for transfers between devices: 11.2 us -> 10.4 us  [moved(): return near(lax.ppermute(array, axis, pairs))]
    unnamed x6 -> x1, local copies, waits for them, and re-layouts: 0.01 us -> 0.65 us
  transfers between devices with their start and end apart: 10 -> 10, of which waited for: 6 -> 5; matrix products, arithmetic and copies ran while one was open for 0% -> 2% of each run, Pallas kernels for 9% -> 10%
where the time goes in v1:
time: 31.1 us; the launch traced here: 30.8 us
  starting transfers between devices  12.1 us (39%)
  waiting for transfers between devices  10.4 us (33%)
  Pallas kernels  6.91 us (22%)
  between operations  0.7 us (2%)
  local copies, waits for them, and re-layouts  0.65 us (2%)
    ppermute x10, starting transfers between devices, moved(): return near(lax.ppermute(array, axis, pairs))  12.1 us
    ppermute x10, waiting for transfers between devices, moved(): return near(lax.ppermute(array, axis, pairs))  10.4 us
    pallas_call x1, Pallas kernels, local_part(): pl.pallas_call(functools.partial(march, steps=steps, shots=shots, depth_c...  1.99 us
    pallas_call x1, Pallas kernels, local_part(): pl.pallas_call(functools.partial(injection, steps=steps, depth_len=depth_...  1.88 us
    pallas_call x1, Pallas kernels, local_part(): pl.pallas_call(functools.partial(pack_fields, steps=steps), in_specs=[HBM...  0.99 us
    pallas_call x1, Pallas kernels, local_part(): pl.pallas_call(functools.partial(pack_model, reach=reach), in_specs=[VMEM...  0.88 us
    pallas_call x1, Pallas kernels, local_part(): pl.pallas_call(functools.partial(finish, steps=steps), in_specs=[VMEM] *...  0.7 us
    unnamed x1, local copies, waits for them, and re-layouts  0.65 us
  transfers between devices with their start and end apart: 10, of which 5 were waited for; matrix products, arithmetic and copies ran while one was open for 2% of the time, Pallas kernels for 10%

profile of v1, /device:TPU:0, one launch (start us, length us, event | category | flops | bytes accessed | tf_op | source)
XLA Modules:
  0.0 30.8 jit_solution(10557292726837221419)
XLA Ops:
  0.6 1.0 %pack_fields.1 = (f32[13,32,128]{2,1,0:T(8,128)S(1)}, f32[13,32,128]{2,1,0:T(8,128)S(1)}) custom-call(f32[1,8,32,128]{3,2,1,0:T(8,128)} %current_ref.3, f32[1,8,32,128]{3,2,1,0:T(8,128)} %previous_ref.3, bf16[4,1,8,32,128]{4,3,2,1,0:T(8,128)(2,1)} %forward_ref.3), custom_call_target="tpu_custom_call" | custom-call | tf_op jit(solution)/shard_map/pack_fields/pallas_call | solution.py:507
  1.6 0.6 %collective-permute-start = (f32[13,32,128]{2,1,0:T(8,128)S(1)}, f32[13,32,128]{2,1,0:T(8,128)S(1)}, u32[]{:S(2)}, u32[]{:S(2)}) collective-permute-start(f32[13,32,128]{2,1,0:T(8,128)S(1)} %get-tuple-element.25), channel_id=1, source_target_pairs={{0,4},{4,0},{8,12},{12,8},{1,5},{5,1},{9,13},{13,9},{2,6},{6,2},{1... | collective-permute-start | bytes 638984 | tf_op jit(solution)/shard_map/ppermute | solution.py:491
  2.2 2.6 %collective-permute-start.1 = (f32[13,32,128]{2,1,0:T(8,128)S(1)}, f32[13,32,128]{2,1,0:T(8,128)S(1)}, u32[]{:S(2)}, u32[]{:S(2)}) collective-permute-start(f32[13,32,128]{2,1,0:T(8,128)S(1)} %get-tuple-element.26), channel_id=1, source_target_pairs={{0,12},{4,8},{8,4},{12,0},{1,13},{5,9},{9,5},{13,1},{2,14},{6,10},... | collective-permute-start | bytes 638984 | tf_op jit(solution)/shard_map/ppermute | solution.py:491
  4.8 0.9 %pack_model.1 = (f32[48,128]{1,0:T(8,128)S(1)}, f32[24,128]{1,0:T(8,128)S(1)}, f32[24,128]{1,0:T(8,128)S(1)}) custom-call(f32[6,4,4,64]{3,2,1,0:T(4,128)} %model_ref.1), custom_call_target="tpu_custom_call" | custom-call | tf_op jit(solution)/shard_map/pack_model/pallas_call | solution.py:497
  5.7 0.1 collective-permute-start.2
  5.8 0.0 collective-permute-start.3
  5.8 1.1 %collective-permute-done.2.first_ref = f32[24,128]{1,0:T(8,128)S(1)} collective-permute-done((f32[24,128]{1,0:T(8,128)S(1)}, f32[24,128]{1,0:T(8,128)S(1)}, u32[]{:S(2)}, u32[]{:S(2)}) %collective-permute-start.2) | collective-permute-done | bytes 12320 | tf_op jit(solution)/shard_map/ppermute | solution.py:491
  6.9 3.7 %collective-permute-done.3.second_ref = f32[24,128]{1,0:T(8,128)S(1)} collective-permute-done((f32[24,128]{1,0:T(8,128)S(1)}, f32[24,128]{1,0:T(8,128)S(1)}, u32[]{:S(2)}, u32[]{:S(2)}) %collective-permute-start.3) | collective-permute-done | bytes 12320 | tf_op jit(solution)/shard_map/ppermute | solution.py:491
  10.6 1.4 %collective-permute-start.4 = (f32[96,128]{1,0:T(8,128)S(1)}, f32[96,128]{1,0:T(8,128)S(1)}, u32[]{:S(2)}, u32[]{:S(2)}) collective-permute-start(f32[96,128]{1,0:T(8,128)S(1)} %join_model.1.refs_0_), channel_id=1, source_target_pairs={{0,1},{1,0},{2,3},{3,2},{4,5},{5,4},{6,7},{7,6},{8,9},{9,8},{10,11... | collective-permute-start | bytes 147464 | tf_op jit(solution)/shard_map/ppermute | solution.py:491
  12.0 2.6 %collective-permute-start.5 = (f32[96,128]{1,0:T(8,128)S(1)}, f32[96,128]{1,0:T(8,128)S(1)}, u32[]{:S(2)}, u32[]{:S(2)}) collective-permute-start(f32[96,128]{1,0:T(8,128)S(1)} %join_model.1.refs_0_), channel_id=1, source_target_pairs={{0,2},{1,3},{2,0},{3,1},{4,6},{5,7},{6,4},{7,5},{8,10},{9,11},{10,... | collective-permute-start | bytes 147464 | tf_op jit(solution)/shard_map/ppermute | solution.py:491
  14.6 0.4 %collective-permute-start.6 = (f32[96,128]{1,0:T(8,128)S(1)}, f32[96,128]{1,0:T(8,128)S(1)}, u32[]{:S(2)}, u32[]{:S(2)}) collective-permute-start(f32[96,128]{1,0:T(8,128)S(1)} %join_model.1.refs_0_), channel_id=1, source_target_pairs={{0,3},{1,2},{2,1},{3,0},{4,7},{5,6},{6,5},{7,4},{8,11},{9,10},{10,... | collective-permute-start | bytes 147464 | tf_op jit(solution)/shard_map/ppermute | solution.py:491
  15.0 1.9 %injection.1 = (f32[4,15,32,128]{3,2,1,0:T(8,128)S(1)}, f32[9,32,128]{2,1,0:T(8,128)S(1)}, f32[1,8,32,128]{3,2,1,0:T(8,128)S(1)}, f32[1,8,32,128]{3,2,1,0:T(8,128)S(1)}, bf16[4,1,8,32,128]{4,3,2,1,0:T(8,128)(2,1)S(1)}) custom-call(s32[4]{0:T(128)} %assign_ref.1, s32[4,3]{1,0:T(4,128)} %source_ref.1, f32[1,4,256]{2,1,0:T(4,128)} %residual_ref.1, ...), custom_call_target="tpu_custom_call" | custom-call | tf_op jit(solution)/shard_map/injection/pallas_call | solution.py:522
  16.9 0.0 collective-permute-done.first_ref
  16.9 0.0 collective-permute-done.1.second_ref
  16.9 0.5 %prepare.1 = (f32[17,48,128]{2,1,0:T(8,128)S(1)}, f32[6,15,32,128]{3,2,1,0:T(8,128)S(1)}, f32[15,32,128]{2,1,0:T(8,128)S(1)}, f32[6,9,32,128]{3,2,1,0:T(8,128)S(1)}, f32[4,9,32,128]{3,2,1,0:T(8,128)S(1)}) custom-call(f32[1,8,32,128]{3,2,1,0:T(8,128)S(1)} %get-tuple-element.22.current_ref, f32[1,8,32,128]{3,2,1,0:T(8,128)S(1)} %get-tuple-element.23.previous_ref, ...), custom_call_target="tpu_custom_call" | custom-call | tf_op jit(solution)/shard_map/prepare/pallas_call | solution.py:559
  17.4 0.0 collective-permute-done.4.refs_1_
  17.4 0.8 %collective-permute-done.5.refs_2_ = f32[96,128]{1,0:T(8,128)S(1)} collective-permute-done((f32[96,128]{1,0:T(8,128)S(1)}, f32[96,128]{1,0:T(8,128)S(1)}, u32[]{:S(2)}, u32[]{:S(2)}) %collective-permute-start.5) | collective-permute-done | bytes 49184 | tf_op jit(solution)/shard_map/ppermute | solution.py:491
  18.1 2.4 %collective-permute-done.6.refs_3_ = f32[96,128]{1,0:T(8,128)S(1)} collective-permute-done((f32[96,128]{1,0:T(8,128)S(1)}, f32[96,128]{1,0:T(8,128)S(1)}, u32[]{:S(2)}, u32[]{:S(2)}) %collective-permute-start.6) | collective-permute-done | bytes 49184 | tf_op jit(solution)/shard_map/ppermute | solution.py:491
  20.5 2.0 %march.1 = (f32[1,8,32,128]{3,2,1,0:T(8,128)S(1)}, f32[48,128]{1,0:T(8,128)S(1)}, f32[48,128]{1,0:T(8,128)S(1)}, f32[48,128]{1,0:T(8,128)S(1)}, f32[48,128]{1,0:T(8,128)S(1)}) custom-call(f32[17,48,128]{2,1,0:T(8,128)S(1)} %get-tuple-element.29.field, f32[6,15,32,128]{3,2,1,0:T(8,128)S(1)} %get-tuple-element.30.start_slopes, ...), custom_call_target="tpu_custom_call" | custom-call | tf_op jit(solution)/shard_map/march/pallas_call | solution.py:586
  22.5 0.1 collective-permute-start.7
  22.6 1.9 %collective-permute-start.8 = (f32[48,128]{1,0:T(8,128)S(1)}, f32[48,128]{1,0:T(8,128)S(1)}, u32[]{:S(2)}, u32[]{:S(2)}) collective-permute-start(f32[48,128]{1,0:T(8,128)S(1)} %get-tuple-element.40), channel_id=1, source_target_pairs={{0,2},{1,3},{2,0},{3,1},{4,6},{5,7},{6,4},{7,5},{8,10},{9,11},{10,... | collective-permute-start | bytes 73736 | tf_op jit(solution)/shard_map/ppermute | solution.py:491
  24.5 2.5 %collective-permute-start.9 = (f32[48,128]{1,0:T(8,128)S(1)}, f32[48,128]{1,0:T(8,128)S(1)}, u32[]{:S(2)}, u32[]{:S(2)}) collective-permute-start(f32[48,128]{1,0:T(8,128)S(1)} %get-tuple-element.41), channel_id=1, source_target_pairs={{0,3},{1,2},{2,1},{3,0},{4,7},{5,6},{6,5},{7,4},{8,11},{9,10},{10,... | collective-permute-start | bytes 73736 | tf_op jit(solution)/shard_map/ppermute | solution.py:491
  27.0 0.7 %copy.10 = f32[1,8,32,128]{3,2,1,0:T(8,128)} copy(f32[1,8,32,128]{3,2,1,0:T(8,128)S(1)} %get-tuple-element.42) | data formatting | bytes 262144
  27.6 0.0 collective-permute-done.7.refs_1_
  27.6 0.0 collective-permute-done.8.refs_2_
  27.6 2.5 %collective-permute-done.9.refs_3_ = f32[48,128]{1,0:T(8,128)S(1)} collective-permute-done((f32[48,128]{1,0:T(8,128)S(1)}, f32[48,128]{1,0:T(8,128)S(1)}, u32[]{:S(2)}, u32[]{:S(2)}) %collective-permute-start.9) | collective-permute-done | bytes 24608 | tf_op jit(solution)/shard_map/ppermute | solution.py:491
  30.1 0.7 %finish.1 = f32[6,4,4,64]{3,2,1,0:T(4,128)} custom-call(f32[48,128]{1,0:T(8,128)S(1)} %get-tuple-element.38.refs_0_, f32[48,128]{1,0:T(8,128)S(1)} %collective-permute-done.7.refs_1_, f32[48,128]{1,0:T(8,128)S(1)} %collective-permute-done.8.refs_2_, f32[48,128]{1,0:T(8,128)S(1)} %collective-permute-done.9.refs_3_), custom_call_target="tpu_custom_call" | custom-call | tf_op jit(solution)/shard_map/finish/pallas_call | solution.py:612
  (1 shorter events, 0.0 us)
Async XLA Ops:
  1.6 15.2 %collective-permute-start = (f32[13,32,128]{2,1,0:T(8,128)S(1)}, f32[13,32,128]{2,1,0:T(8,128)S(1)}, u32[]{:S(2)}, u32[]{:S(2)}) collective-permute-start(f32[13,32,128]{2,1,0:T(8,128)S(1)} %get-tuple-element.25), channel_id=1, source_target_pairs={{0,4},{4,0},{8,12},{12,8},{1,5},{5,1},{9,13},{13,9},{2,6},{6,2},{1... | collective-permute-start | bytes 638984 | tf_op jit(solution)/shard_map/ppermute | solution.py:491
  2.2 14.7 %collective-permute-start.1 = (f32[13,32,128]{2,1,0:T(8,128)S(1)}, f32[13,32,128]{2,1,0:T(8,128)S(1)}, u32[]{:S(2)}, u32[]{:S(2)}) collective-permute-start(f32[13,32,128]{2,1,0:T(8,128)S(1)} %get-tuple-element.26), channel_id=1, source_target_pairs={{0,12},{4,8},{8,4},{12,0},{1,13},{5,9},{9,5},{13,1},{2,14},{6,10},... | collective-permute-start | bytes 638984 | tf_op jit(solution)/shard_map/ppermute | solution.py:491
  5.7 1.2 %collective-permute-start.2 = (f32[24,128]{1,0:T(8,128)S(1)}, f32[24,128]{1,0:T(8,128)S(1)}, u32[]{:S(2)}, u32[]{:S(2)}) collective-permute-start(f32[24,128]{1,0:T(8,128)S(1)} %get-tuple-element.35), channel_id=1, source_target_pairs={{0,4},{4,0},{8,12},{12,8},{1,5},{5,1},{9,13},{13,9},{2,6},{6,2},{1... | collective-permute-start | bytes 36872 | tf_op jit(solution)/shard_map/ppermute | solution.py:491
  5.8 4.8 %collective-permute-start.3 = (f32[24,128]{1,0:T(8,128)S(1)}, f32[24,128]{1,0:T(8,128)S(1)}, u32[]{:S(2)}, u32[]{:S(2)}) collective-permute-start(f32[24,128]{1,0:T(8,128)S(1)} %get-tuple-element.36), channel_id=1, source_target_pairs={{0,12},{4,8},{8,4},{12,0},{1,13},{5,9},{9,5},{13,1},{2,14},{6,10},... | collective-permute-start | bytes 36872 | tf_op jit(solution)/shard_map/ppermute | solution.py:491
  10.6 6.8 %collective-permute-start.4 = (f32[96,128]{1,0:T(8,128)S(1)}, f32[96,128]{1,0:T(8,128)S(1)}, u32[]{:S(2)}, u32[]{:S(2)}) collective-permute-start(f32[96,128]{1,0:T(8,128)S(1)} %join_model.1.refs_0_), channel_id=1, source_target_pairs={{0,1},{1,0},{2,3},{3,2},{4,5},{5,4},{6,7},{7,6},{8,9},{9,8},{10,11... | collective-permute-start | bytes 147464 | tf_op jit(solution)/shard_map/ppermute | solution.py:491
  12.0 6.1 %collective-permute-start.5 = (f32[96,128]{1,0:T(8,128)S(1)}, f32[96,128]{1,0:T(8,128)S(1)}, u32[]{:S(2)}, u32[]{:S(2)}) collective-permute-start(f32[96,128]{1,0:T(8,128)S(1)} %join_model.1.refs_0_), channel_id=1, source_target_pairs={{0,2},{1,3},{2,0},{3,1},{4,6},{5,7},{6,4},{7,5},{8,10},{9,11},{10,... | collective-permute-start | bytes 147464 | tf_op jit(solution)/shard_map/ppermute | solution.py:491
  14.6 5.9 %collective-permute-start.6 = (f32[96,128]{1,0:T(8,128)S(1)}, f32[96,128]{1,0:T(8,128)S(1)}, u32[]{:S(2)}, u32[]{:S(2)}) collective-permute-start(f32[96,128]{1,0:T(8,128)S(1)} %join_model.1.refs_0_), channel_id=1, source_target_pairs={{0,3},{1,2},{2,1},{3,0},{4,7},{5,6},{6,5},{7,4},{8,11},{9,10},{10,... | collective-permute-start | bytes 147464 | tf_op jit(solution)/shard_map/ppermute | solution.py:491
  22.5 5.1 %collective-permute-start.7 = (f32[48,128]{1,0:T(8,128)S(1)}, f32[48,128]{1,0:T(8,128)S(1)}, u32[]{:S(2)}, u32[]{:S(2)}) collective-permute-start(f32[48,128]{1,0:T(8,128)S(1)} %get-tuple-element.39), channel_id=1, source_target_pairs={{0,1},{1,0},{2,3},{3,2},{4,5},{5,4},{6,7},{7,6},{8,9},{9,8},{10,11... | collective-permute-start | bytes 73736 | tf_op jit(solution)/shard_map/ppermute | solution.py:491
  22.6 5.0 %collective-permute-start.8 = (f32[48,128]{1,0:T(8,128)S(1)}, f32[48,128]{1,0:T(8,128)S(1)}, u32[]{:S(2)}, u32[]{:S(2)}) collective-permute-start(f32[48,128]{1,0:T(8,128)S(1)} %get-tuple-element.40), channel_id=1, source_target_pairs={{0,2},{1,3},{2,0},{3,1},{4,6},{5,7},{6,4},{7,5},{8,10},{9,11},{10,... | collective-permute-start | bytes 73736 | tf_op jit(solution)/shard_map/ppermute | solution.py:491
  24.5 5.6 %collective-permute-start.9 = (f32[48,128]{1,0:T(8,128)S(1)}, f32[48,128]{1,0:T(8,128)S(1)}, u32[]{:S(2)}, u32[]{:S(2)}) collective-permute-start(f32[48,128]{1,0:T(8,128)S(1)} %get-tuple-element.41), channel_id=1, source_target_pairs={{0,3},{1,2},{2,1},{3,0},{4,7},{5,6},{6,5},{7,4},{8,11},{9,10},{10,... | collective-permute-start | bytes 73736 | tf_op jit(solution)/shard_map/ppermute | solution.py:491

commit v2 on v1

--- a/solution.py
+++ b/solution.py
@@ -34,8 +34,10 @@
         parts.append(left.astype(jnp.bfloat16))
         left = left - parts[-1].astype(jnp.float32)
     product = functools.partial(jnp.dot, preferred_element_type=jnp.float32)
-    stacked = jnp.concatenate([right, right], axis=0)
-    return product(jnp.concatenate(parts[:2], axis=1), stacked) + product(parts[2], right)
+    if right.shape[0] == 128:
+        stacked = jnp.concatenate([right, right], axis=0)
+        return product(jnp.concatenate(parts[:2], axis=1), stacked) + product(parts[2], right)
+    return product(parts[0], right) + product(parts[1], right) + product(parts[2], right)
 
 
 def even_depth():
@@ -205,33 +207,40 @@
         load.wait()
 
 
-def slopes_at(field, across, bend, e, rows):
+def slopes_at(field, lines, e, rows):
+    across, bend, slant, bow = lines
     inner = slice(PAD, PAD + rows)
     before = slice(PAD - 1, PAD - 1 + rows)
     after = slice(PAD + 1, PAD + 1 + rows)
     twice = 2.0 * field[e, inner, :]
     slopes = [
         field[e + 1, inner, :] - twice + field[e - 1, inner, :],
-        field[e, after, :] - twice + field[e, before, :],
+        bow[e],
         bend[e],
-        (field[e + 1, after, :] - field[e + 1, before, :])
-        - (field[e - 1, after, :] - field[e - 1, before, :]),
+        slant[e + 1] - slant[e - 1],
         across[e + 1, inner, :] - across[e - 1, inner, :],
         across[e, after, :] - across[e, before, :],
     ]
     return twice, slopes
 
 
-def columns_of(field, across, bend, lowest, highest, rows):
+def differences(field, lines, lowest, highest, rows):
+    across, bend, slant, bow = lines
     columns = field.shape[2]
     inner = slice(PAD, PAD + rows)
     lane = lax.broadcasted_iota(jnp.int32, (rows, columns), 1)
     for e in range(lowest, highest + 1):
         value = field[e, inner, :]
+        twice = 2.0 * value
         right = jnp.where(lane == columns - 1, 0.0, pltpu.roll(value, columns - 1, 1))
         left = jnp.where(lane == 0, 0.0, pltpu.roll(value, 1, 1))
         across[e, inner, :] = right - left
-        bend[e] = right + left - 2.0 * value
+        bend[e] = right + left - twice
+        before = field[e, PAD - 1 : PAD - 1 + rows, :]
+        after = field[e, PAD + 1 : PAD + 1 + rows, :]
+        slant[e] = after - before
+        if lowest < e < highest:
+            bow[e] = after + before - twice
 
 
 def clear_rim(field, rows):
@@ -256,6 +265,8 @@
     weights,
     across,
     bend,
+    slant,
+    bow,
     older,
     *,
     steps,
@@ -308,14 +319,35 @@
         )
         older[up + depth_len : height] = jnp.zeros((down,) + current_ref.shape[2:], jnp.float32)
 
-    columns_of(field, across, bend, 0, height - 1, rows)
+    lines = (across, bend, slant, bow)
+    differences(field, lines, 0, height - 1, rows)
     for e in range(1, height - 1):
-        twice, slopes = slopes_at(field, across, bend, e, rows)
+        twice, slopes = slopes_at(field, lines, e, rows)
         for k, slope in enumerate(slopes):
             start_slopes[k, e - 1] = slope
             if up - 1 <= e < up + depth_len:
                 start_totals[k, e - up + 1] = weights[0, e - up + 1] * slope
         start_base[e - 1] = twice - older[e] + added_ref[0, e - 1]
+
+
+def change_at(even_rows, odd_rows, slopes, z):
+    table = even_rows if z % 2 == 0 else odd_rows
+    change = table[z // 2, 0] * slopes[0]
+    for k in range(1, len(slopes)):
+        change = change + table[z // 2, k] * slopes[k]
+    return change
+
+
+def last_update(*refs, steps, reach):
+    now, old, even_rows, odd_rows, added_ref, final_ref, *lines = refs
+    depth_len, rows, _ = final_ref.shape[1:]
+    up = steps + 1
+    clear_rim(lines[0], rows)
+    differences(now, lines, up - 1, up + depth_len, rows)
+    for e in range(up, up + depth_len):
+        twice, slopes = slopes_at(now, lines, e, rows)
+        base = twice - old[e, PAD : PAD + rows, :] + added_ref[steps - 1, e - 1]
+        final_ref[0, e - up] = base + change_at(even_rows, odd_rows, slopes, e - up + 2 * reach)
 
 
 def march(
@@ -331,14 +363,13 @@
     depth_count,
     reach,
 ):
-    gathered = refs[:shots]
-    final_ref = refs[shots]
-    chunks = refs[shots + 1 : 2 * shots + 1]
-    blocks, packed, coarse, even_rows, odd_rows, ones, twos, across, bend, totals, result = refs[
-        2 * shots + 1 :
+    gathered, chunks = refs[:shots], refs[shots : 2 * shots]
+    ones, twos, even_rows, odd_rows, blocks, packed, coarse, *lines, totals, result = refs[
+        2 * shots :
     ]
-    depth_len, rows, columns = final_ref.shape[1:]
-    channels = start_slopes.shape[0]
+    across = lines[0]
+    rows, columns = start_base.shape[1:]
+    channels, depth_len = start_slopes.shape[0], weights.shape[1] - 1
     up, down = steps + 1, steps
     height = up + depth_len + down
     depth_index = lax.axis_index("depth")
@@ -386,70 +417,64 @@
         now = field if i == 0 else (ones if i % 2 else twos)
         old = field if i == 1 else (twos if i % 2 else ones)
         new = twos if i % 2 else ones
+        last = i == steps - 1
         if i > 0:
-            columns_of(now, across, bend, i, height - 1 - i, rows)
+            differences(now, lines, i, height - 1 - i, rows)
         for e in range(i + 1, height - 1 - i):
             counted = up - 1 <= e < up + depth_len and i > 0
-            stepped = i < steps - 1 or up <= e < up + depth_len
-            if not (counted or stepped):
+            if last and not counted:
                 continue
             if i == 0:
                 slopes = [start_slopes[k, e - 1] for k in range(channels)]
                 base = start_base[e - 1]
             else:
-                twice, slopes = slopes_at(now, across, bend, e, rows)
+                twice, slopes = slopes_at(now, lines, e, rows)
             if counted:
                 weight = weights[i, e - up + 1]
                 for k in range(channels):
                     so_far = start_totals if i == 1 else totals
                     totals[k, e - up + 1] = so_far[k, e - up + 1] + weight * slopes[k]
-            if stepped:
+            if not last:
                 if i > 0:
                     base = twice - old[e, inner, :] + added_ref[i, e - 1]
-                z = e - up + 2 * reach
-                table = even_rows if z % 2 == 0 else odd_rows
-                change = table[z // 2, 0] * slopes[0]
-                for k in range(1, channels):
-                    change = change + table[z // 2, k] * slopes[k]
-                updated = base + change
+                updated = base + change_at(even_rows, odd_rows, slopes, e - up + 2 * reach)
                 if e < up:
                     updated = jnp.where(is_top, 0.0, updated)
                 if e >= up + depth_len:
                     updated = jnp.where(is_last, 0.0, updated)
-                if i < steps - 1:
-                    new[e, inner, :] = updated
-                else:
-                    final_ref[0, e - up] = updated
-    if steps == 1:
-        totals[...] = start_totals[...]
-
+                new[e, inner, :] = updated
+
+    gather = refine.T
+    none = jnp.zeros_like(gather)
+    gather_pair = jnp.concatenate(
+        [
+            jnp.concatenate([gather, none], axis=1),
+            jnp.concatenate([none, 0.25 * gather], axis=1),
+        ],
+        axis=0,
+    )
     depth_half = depth_len // 2
     line = lax.broadcasted_iota(jnp.int32, (coarse_rows, columns), 0)
-    for k in range(channels):
-        for z in range(depth_half):
-            slot = (k * depth_half + z) % result.shape[0]
-            result[slot] = totals[k, 2 * z + 1] + totals[k, 2 * z] + totals[k, 2 * z + 2]
+    for z in range(depth_half):
+        for channel in range(channels):
+            slot = (z * channels + channel) % result.shape[0]
+            result[slot] = (
+                totals[channel, 2 * z + 1] + totals[channel, 2 * z] + totals[channel, 2 * z + 2]
+            )
             even = result[slot, pl.ds(0, coarse_rows, stride=2), :]
             odd = 0.5 * result[slot, pl.ds(1, coarse_rows, stride=2), :]
-            ones[slot, PAD : PAD + coarse_rows, :] = odd
+            across[slot, PAD : PAD + coarse_rows, :] = odd
             tail = jnp.where(line == coarse_rows - 1, odd, 0.0)
-            value = even + odd + ones[slot, PAD - 1 : PAD - 1 + coarse_rows, :] + tail
-            at = (k * depth_half + z) * coarse_rows
-            blocks[at : at + coarse_rows, :] = value
-    rows_half = half * depth_half * coarse_rows
-    gather = refine.T
-    none = jnp.zeros_like(gather)
-    packed[...] = exact_dot(
-        blocks[0:rows_half, :], jnp.concatenate([gather, none], axis=1)
-    ) + exact_dot(
-        blocks[rows_half : 2 * rows_half, :], jnp.concatenate([none, 0.25 * gather], axis=1)
-    )
+            value = even + odd + across[slot, PAD - 1 : PAD - 1 + coarse_rows, :] + tail
+            at, side = (channel % half) * coarse_rows, channel // half * columns
+            blocks[z, at : at + coarse_rows, side : side + columns] = value
+        packed[z] = exact_dot(blocks[z], gather_pair)
     for j in range(shots):
         start = (shot_index ^ j) * share
-        for layer in range(half * depth_half):
-            chunks[j][layer * share : (layer + 1) * share, :] = packed[
-                pl.ds(layer * coarse_rows + start, share), :
-            ]
+        for k in range(half):
+            for z in range(depth_half):
+                at = (k * depth_half + z) * share
+                chunks[j][at : at + share, :] = packed[z, pl.ds(k * coarse_rows + start, share), :]
 
 
 def finish(*refs, steps):
@@ -478,7 +503,7 @@
     reach = (steps + 1) // 2
     assert shots_here == 1 and depth_count % 2 == 0 and shots & (shots - 1) == 0
     assert channels == 6 and 2 * coarse_columns == columns
-    assert depth_len > steps and coarse_len >= reach and share * shots * 2 == rows
+    assert steps % 2 == 0 and steps > 2 and depth_len > steps and coarse_len >= reach and share * shots * 2 == rows
     f32 = jnp.float32
     shape = lambda *dims: jax.ShapeDtypeStruct(dims, f32)
     local = lambda *dims: pltpu.VMEM(dims, f32)
@@ -568,9 +593,11 @@
             local(steps, depth_len + 1, rows, columns),
         ],
         scratch_shapes=[
-            pltpu.VMEM((height, padded, columns), f32),
-            pltpu.VMEM((height, rows, columns), f32),
-            pltpu.VMEM((height, rows, columns), f32),
+            local(height, padded, columns),
+            local(height, rows, columns),
+            local(height, rows, columns),
+            local(height, rows, columns),
+            local(height, rows, columns),
         ],
         name="prepare",
         compiler_params=LIMIT,
@@ -583,31 +610,44 @@
     )
     layers = coarse_len + 2 * reach
     chunk = local(half * coarse_len * share, columns)
-    final, *chunks = pl.pallas_call(
+    lines = [
+        local(height, padded, columns),
+        local(height, rows, columns),
+        local(height, rows, columns),
+        local(height, rows, columns),
+    ]
+    outs = pl.pallas_call(
         functools.partial(march, steps=steps, shots=shots, depth_count=depth_count, reach=reach),
         in_specs=[VMEM] * (6 + shots),
-        out_specs=[VMEM] * (1 + shots),
-        out_shape=[local(1, depth_len, rows, columns)] + [chunk] * shots,
+        out_specs=[VMEM] * (shots + 4),
+        out_shape=[chunk] * shots
+        + [
+            local(height, padded, columns),
+            local(height, padded, columns),
+            local(layers, channels, rows, columns),
+            local(layers - 1, channels, rows, columns),
+        ],
         scratch_shapes=[
-            pltpu.VMEM((channels * coarse_len * rows // 2, columns), f32),
-            pltpu.VMEM((half * coarse_len * rows // 2, columns), f32),
-            pltpu.VMEM((layers, channels, rows // 2 + PAD, columns), f32),
-            pltpu.VMEM((layers, channels, rows, columns), f32),
-            pltpu.VMEM((layers - 1, channels, rows, columns), f32),
-            pltpu.VMEM((height, padded, columns), f32),
-            pltpu.VMEM((height, padded, columns), f32),
-            pltpu.VMEM((height, padded, columns), f32),
-            pltpu.VMEM((height, rows, columns), f32),
-            pltpu.VMEM((channels, depth_len + 1, rows, columns), f32),
-            pltpu.VMEM((4, rows, columns), f32),
+            local(coarse_len, half * rows // 2, 2 * columns),
+            local(coarse_len, half * rows // 2, columns),
+            local(layers, channels, rows // 2 + PAD, columns),
+            *lines,
+            local(channels, depth_len + 1, rows, columns),
+            local(12, rows, columns),
         ],
         name="march",
         compiler_params=LIMIT,
-    )(
-        *map(near, prepared),
-        near(added),
-        *gathered,
-    )
+    )(*map(near, prepared), near(added), *gathered)
+    chunks, kept = outs[:shots], outs[shots:]
+    final = pl.pallas_call(
+        functools.partial(last_update, steps=steps, reach=reach),
+        in_specs=[VMEM] * 5,
+        out_specs=VMEM,
+        out_shape=shape(1, depth_len, rows, columns),
+        scratch_shapes=lines,
+        name="last_update",
+        compiler_params=LIMIT,
+    )(*map(near, kept), near(added))
     parts = [near(chunks[0])] + [swap(chunks[j], j) for j in range(1, shots)]
     gradients = pl.pallas_call(
         functools.partial(finish, steps=steps),

time: 31.1 us -> 30.7 us (0.987)
  Pallas kernels: 6.91 us -> 7.69 us
  local copies, waits for them, and re-layouts: 0.65 us -> 0 us
  waiting for transfers between devices: 10.4 us -> 9.9 us
    pallas_call x0 -> x1, Pallas kernels: none -> 0.87 us  [local_part(): pl.pallas_call(functools.partial(last_update, steps=steps, reach=reach),...]
    unnamed x1 -> x0, local copies, waits for them, and re-layouts: 0.65 us -> none
    ppermute x10, waiting for transfers between devices: 10.4 us -> 9.9 us  [moved(): return near(lax.ppermute(array, axis, pairs))]
  transfers between devices with their start and end apart: 10 -> 10, of which waited for: 5 -> 5; matrix products, arithmetic and copies ran while one was open for 2% -> 0% of each run, Pallas kernels for 10% -> 13%
where the time goes in v2:
time: 30.7 us; the launch traced here: 30.4 us
  starting transfers between devices  12.1 us (39%)
  waiting for transfers between devices  9.9 us (32%)
  Pallas kernels  7.69 us (25%)
  between operations  0.69 us (2%)
    ppermute x10, starting transfers between devices, moved(): return near(lax.ppermute(array, axis, pairs))  12.1 us
    ppermute x10, waiting for transfers between devices, moved(): return near(lax.ppermute(array, axis, pairs))  9.9 us
    pallas_call x1, Pallas kernels, local_part(): pl.pallas_call(functools.partial(march, steps=steps, shots=shots, depth_c...  1.95 us
    pallas_call x1, Pallas kernels, local_part(): pl.pallas_call(functools.partial(injection, steps=steps, depth_len=depth_...  1.88 us
    pallas_call x1, Pallas kernels, local_part(): pl.pallas_call(functools.partial(pack_fields, steps=steps), in_specs=[HBM...  0.99 us
    pallas_call x1, Pallas kernels, local_part(): pl.pallas_call(functools.partial(pack_model, reach=reach), in_specs=[VMEM...  0.88 us
    pallas_call x1, Pallas kernels, local_part(): pl.pallas_call(functools.partial(last_update, steps=steps, reach=reach),...  0.87 us
    pallas_call x1, Pallas kernels, local_part(): pl.pallas_call(functools.partial(finish, steps=steps), in_specs=[VMEM] *...  0.7 us
  transfers between devices with their start and end apart: 10, of which 5 were waited for; matrix products, arithmetic and copies ran while one was open for 0% of the time, Pallas kernels for 13%

profile of v2, /device:TPU:0, one launch (start us, length us, event | category | flops | bytes accessed | tf_op | source)
XLA Modules:
  0.0 30.4 jit_solution(717873347625873569)
XLA Ops:
  0.6 1.0 %pack_fields.1 = (f32[13,32,128]{2,1,0:T(8,128)S(1)}, f32[13,32,128]{2,1,0:T(8,128)S(1)}) custom-call(f32[1,8,32,128]{3,2,1,0:T(8,128)} %current_ref.3, f32[1,8,32,128]{3,2,1,0:T(8,128)} %previous_ref.3, bf16[4,1,8,32,128]{4,3,2,1,0:T(8,128)(2,1)} %forward_ref.3), custom_call_target="tpu_custom_call" | custom-call | tf_op jit(solution)/shard_map/pack_fields/pallas_call | solution.py:532
  1.6 0.6 %collective-permute-start = (f32[13,32,128]{2,1,0:T(8,128)S(1)}, f32[13,32,128]{2,1,0:T(8,128)S(1)}, u32[]{:S(2)}, u32[]{:S(2)}) collective-permute-start(f32[13,32,128]{2,1,0:T(8,128)S(1)} %get-tuple-element.28), channel_id=1, source_target_pairs={{0,4},{4,0},{8,12},{12,8},{1,5},{5,1},{9,13},{13,9},{2,6},{6,2},{1... | collective-permute-start | bytes 638984 | tf_op jit(solution)/shard_map/ppermute | solution.py:516
  2.2 2.6 %collective-permute-start.1 = (f32[13,32,128]{2,1,0:T(8,128)S(1)}, f32[13,32,128]{2,1,0:T(8,128)S(1)}, u32[]{:S(2)}, u32[]{:S(2)}) collective-permute-start(f32[13,32,128]{2,1,0:T(8,128)S(1)} %get-tuple-element.29), channel_id=1, source_target_pairs={{0,12},{4,8},{8,4},{12,0},{1,13},{5,9},{9,5},{13,1},{2,14},{6,10},... | collective-permute-start | bytes 638984 | tf_op jit(solution)/shard_map/ppermute | solution.py:516
  4.8 0.9 %pack_model.1 = (f32[48,128]{1,0:T(8,128)S(1)}, f32[24,128]{1,0:T(8,128)S(1)}, f32[24,128]{1,0:T(8,128)S(1)}) custom-call(f32[6,4,4,64]{3,2,1,0:T(4,128)} %model_ref.1), custom_call_target="tpu_custom_call" | custom-call | tf_op jit(solution)/shard_map/pack_model/pallas_call | solution.py:522
  5.7 0.1 collective-permute-start.2
  5.8 0.0 collective-permute-start.3
  5.8 1.1 %collective-permute-done.2.first_ref = f32[24,128]{1,0:T(8,128)S(1)} collective-permute-done((f32[24,128]{1,0:T(8,128)S(1)}, f32[24,128]{1,0:T(8,128)S(1)}, u32[]{:S(2)}, u32[]{:S(2)}) %collective-permute-start.2) | collective-permute-done | bytes 12320 | tf_op jit(solution)/shard_map/ppermute | solution.py:516
  6.9 3.7 %collective-permute-done.3.second_ref = f32[24,128]{1,0:T(8,128)S(1)} collective-permute-done((f32[24,128]{1,0:T(8,128)S(1)}, f32[24,128]{1,0:T(8,128)S(1)}, u32[]{:S(2)}, u32[]{:S(2)}) %collective-permute-start.3) | collective-permute-done | bytes 12320 | tf_op jit(solution)/shard_map/ppermute | solution.py:516
  10.6 3.5 %collective-permute-start.6 = (f32[96,128]{1,0:T(8,128)S(1)}, f32[96,128]{1,0:T(8,128)S(1)}, u32[]{:S(2)}, u32[]{:S(2)}) collective-permute-start(f32[96,128]{1,0:T(8,128)S(1)} %join_model.1.refs_0_), channel_id=1, source_target_pairs={{0,3},{1,2},{2,1},{3,0},{4,7},{5,6},{6,5},{7,4},{8,11},{9,10},{10,... | collective-permute-start | bytes 147464 | tf_op jit(solution)/shard_map/ppermute | solution.py:516
  14.1 0.0 collective-permute-start.5
  14.1 0.9 %collective-permute-start.4 = (f32[96,128]{1,0:T(8,128)S(1)}, f32[96,128]{1,0:T(8,128)S(1)}, u32[]{:S(2)}, u32[]{:S(2)}) collective-permute-start(f32[96,128]{1,0:T(8,128)S(1)} %join_model.1.refs_0_), channel_id=1, source_target_pairs={{0,1},{1,0},{2,3},{3,2},{4,5},{5,4},{6,7},{7,6},{8,9},{9,8},{10,11... | collective-permute-start | bytes 147464 | tf_op jit(solution)/shard_map/ppermute | solution.py:516
  15.0 1.9 %injection.1 = (f32[4,15,32,128]{3,2,1,0:T(8,128)S(1)}, f32[9,32,128]{2,1,0:T(8,128)S(1)}, f32[1,8,32,128]{3,2,1,0:T(8,128)S(1)}, f32[1,8,32,128]{3,2,1,0:T(8,128)S(1)}, bf16[4,1,8,32,128]{4,3,2,1,0:T(8,128)(2,1)S(1)}) custom-call(s32[4]{0:T(128)} %assign_ref.1, s32[4,3]{1,0:T(4,128)} %source_ref.1, f32[1,4,256]{2,1,0:T(4,128)} %residual_ref.1, ...), custom_call_target="tpu_custom_call" | custom-call | tf_op jit(solution)/shard_map/injection/pallas_call | solution.py:547
  16.9 0.0 collective-permute-done.first_ref
  16.9 0.0 collective-permute-done.1.second_ref
  16.9 0.4 %prepare.1 = (f32[17,48,128]{2,1,0:T(8,128)S(1)}, f32[6,15,32,128]{3,2,1,0:T(8,128)S(1)}, f32[15,32,128]{2,1,0:T(8,128)S(1)}, f32[6,9,32,128]{3,2,1,0:T(8,128)S(1)}, f32[4,9,32,128]{3,2,1,0:T(8,128)S(1)}) custom-call(f32[1,8,32,128]{3,2,1,0:T(8,128)S(1)} %get-tuple-element.25.current_ref, f32[1,8,32,128]{3,2,1,0:T(8,128)S(1)} %get-tuple-element.26.previous_ref, ...), custom_call_target="tpu_custom_call" | custom-call | tf_op jit(solution)/shard_map/prepare/pallas_call | solution.py:584
  17.3 0.0 collective-permute-done.6.refs_3_
  17.3 1.9 %collective-permute-done.5.refs_2_ = f32[96,128]{1,0:T(8,128)S(1)} collective-permute-done((f32[96,128]{1,0:T(8,128)S(1)}, f32[96,128]{1,0:T(8,128)S(1)}, u32[]{:S(2)}, u32[]{:S(2)}) %collective-permute-start.5) | collective-permute-done | bytes 49184 | tf_op jit(solution)/shard_map/ppermute | solution.py:516
  19.2 0.0 collective-permute-done.4.refs_1_
  19.2 2.0 %march.1 = (f32[48,128]{1,0:T(8,128)S(1)}, f32[48,128]{1,0:T(8,128)S(1)}, f32[48,128]{1,0:T(8,128)S(1)}, f32[48,128]{1,0:T(8,128)S(1)}, f32[17,48,128]{2,1,0:T(8...) custom-call(f32[17,48,128]{2,1,0:T(8,128)S(1)} %get-tuple-element.32.field, ...), custom_call_target="tpu_custom_call" | custom-call | tf_op jit(solution)/shard_map/march/pallas_call | solution.py:619
  21.2 1.2 %collective-permute-start.7 = (f32[48,128]{1,0:T(8,128)S(1)}, f32[48,128]{1,0:T(8,128)S(1)}, u32[]{:S(2)}, u32[]{:S(2)}) collective-permute-start(f32[48,128]{1,0:T(8,128)S(1)} %get-tuple-element.45), channel_id=1, source_target_pairs={{0,1},{1,0},{2,3},{3,2},{4,5},{5,4},{6,7},{7,6},{8,9},{9,8},{10,11... | collective-permute-start | bytes 73736 | tf_op jit(solution)/shard_map/ppermute | solution.py:516
  22.3 1.8 %collective-permute-start.8 = (f32[48,128]{1,0:T(8,128)S(1)}, f32[48,128]{1,0:T(8,128)S(1)}, u32[]{:S(2)}, u32[]{:S(2)}) collective-permute-start(f32[48,128]{1,0:T(8,128)S(1)} %get-tuple-element.46), channel_id=1, source_target_pairs={{0,2},{1,3},{2,0},{3,1},{4,6},{5,7},{6,4},{7,5},{8,10},{9,11},{10,... | collective-permute-start | bytes 73736 | tf_op jit(solution)/shard_map/ppermute | solution.py:516
  24.1 1.5 %collective-permute-start.9 = (f32[48,128]{1,0:T(8,128)S(1)}, f32[48,128]{1,0:T(8,128)S(1)}, u32[]{:S(2)}, u32[]{:S(2)}) collective-permute-start(f32[48,128]{1,0:T(8,128)S(1)} %get-tuple-element.47), channel_id=1, source_target_pairs={{0,3},{1,2},{2,1},{3,0},{4,7},{5,6},{6,5},{7,4},{8,11},{9,10},{10,... | collective-permute-start | bytes 73736 | tf_op jit(solution)/shard_map/ppermute | solution.py:516
  25.6 0.9 %last_update.1 = f32[1,8,32,128]{3,2,1,0:T(8,128)} custom-call(f32[17,48,128]{2,1,0:T(8,128)S(1)} %get-tuple-element.40.refs_0_, f32[17,48,128]{2,1,0:T(8,128)S(1)} %get-tuple-element.41.refs_1_, f32[8,6,32,128]{3,2,1,0:T(8,128)S(1)} %get-tuple-element.42.refs_2_, f32[7,6,32,128]{3,2,1,0:T(8,128)S(1)} %get-tuple-element.43.refs_3_, ...), custom_call_target="tpu_custom_call" | custom-call | tf_op jit(solution)/shard_map/last_update/pallas_call | solution.py:642
  26.5 0.0 collective-permute-done.7.refs_1_
  26.5 0.6 %collective-permute-done.8.refs_2_ = f32[48,128]{1,0:T(8,128)S(1)} collective-permute-done((f32[48,128]{1,0:T(8,128)S(1)}, f32[48,128]{1,0:T(8,128)S(1)}, u32[]{:S(2)}, u32[]{:S(2)}) %collective-permute-start.8) | collective-permute-done | bytes 24608 | tf_op jit(solution)/shard_map/ppermute | solution.py:516
  27.0 2.7 %collective-permute-done.9.refs_3_ = f32[48,128]{1,0:T(8,128)S(1)} collective-permute-done((f32[48,128]{1,0:T(8,128)S(1)}, f32[48,128]{1,0:T(8,128)S(1)}, u32[]{:S(2)}, u32[]{:S(2)}) %collective-permute-start.9) | collective-permute-done | bytes 24608 | tf_op jit(solution)/shard_map/ppermute | solution.py:516
  29.7 0.7 %finish.1 = f32[6,4,4,64]{3,2,1,0:T(4,128)} custom-call(f32[48,128]{1,0:T(8,128)S(1)} %get-tuple-element.44.refs_0_, f32[48,128]{1,0:T(8,128)S(1)} %collective-permute-done.7.refs_1_, f32[48,128]{1,0:T(8,128)S(1)} %collective-permute-done.8.refs_2_, f32[48,128]{1,0:T(8,128)S(1)} %collective-permute-done.9.refs_3_), custom_call_target="tpu_custom_call" | custom-call | tf_op jit(solution)/shard_map/finish/pallas_call | solution.py:652
  (1 shorter events, 0.0 us)
Async XLA Ops:
  1.6 15.2 %collective-permute-start = (f32[13,32,128]{2,1,0:T(8,128)S(1)}, f32[13,32,128]{2,1,0:T(8,128)S(1)}, u32[]{:S(2)}, u32[]{:S(2)}) collective-permute-start(f32[13,32,128]{2,1,0:T(8,128)S(1)} %get-tuple-element.28), channel_id=1, source_target_pairs={{0,4},{4,0},{8,12},{12,8},{1,5},{5,1},{9,13},{13,9},{2,6},{6,2},{1... | collective-permute-start | bytes 638984 | tf_op jit(solution)/shard_map/ppermute | solution.py:516
  2.2 14.7 %collective-permute-start.1 = (f32[13,32,128]{2,1,0:T(8,128)S(1)}, f32[13,32,128]{2,1,0:T(8,128)S(1)}, u32[]{:S(2)}, u32[]{:S(2)}) collective-permute-start(f32[13,32,128]{2,1,0:T(8,128)S(1)} %get-tuple-element.29), channel_id=1, source_target_pairs={{0,12},{4,8},{8,4},{12,0},{1,13},{5,9},{9,5},{13,1},{2,14},{6,10},... | collective-permute-start | bytes 638984 | tf_op jit(solution)/shard_map/ppermute | solution.py:516
  5.7 1.2 %collective-permute-start.2 = (f32[24,128]{1,0:T(8,128)S(1)}, f32[24,128]{1,0:T(8,128)S(1)}, u32[]{:S(2)}, u32[]{:S(2)}) collective-permute-start(f32[24,128]{1,0:T(8,128)S(1)} %get-tuple-element.38), channel_id=1, source_target_pairs={{0,4},{4,0},{8,12},{12,8},{1,5},{5,1},{9,13},{13,9},{2,6},{6,2},{1... | collective-permute-start | bytes 36872 | tf_op jit(solution)/shard_map/ppermute | solution.py:516
  5.8 4.8 %collective-permute-start.3 = (f32[24,128]{1,0:T(8,128)S(1)}, f32[24,128]{1,0:T(8,128)S(1)}, u32[]{:S(2)}, u32[]{:S(2)}) collective-permute-start(f32[24,128]{1,0:T(8,128)S(1)} %get-tuple-element.39), channel_id=1, source_target_pairs={{0,12},{4,8},{8,4},{12,0},{1,13},{5,9},{9,5},{13,1},{2,14},{6,10},... | collective-permute-start | bytes 36872 | tf_op jit(solution)/shard_map/ppermute | solution.py:516
  10.6 6.7 %collective-permute-start.6 = (f32[96,128]{1,0:T(8,128)S(1)}, f32[96,128]{1,0:T(8,128)S(1)}, u32[]{:S(2)}, u32[]{:S(2)}) collective-permute-start(f32[96,128]{1,0:T(8,128)S(1)} %join_model.1.refs_0_), channel_id=1, source_target_pairs={{0,3},{1,2},{2,1},{3,0},{4,7},{5,6},{6,5},{7,4},{8,11},{9,10},{10,... | collective-permute-start | bytes 147464 | tf_op jit(solution)/shard_map/ppermute | solution.py:516
  14.1 5.1 %collective-permute-start.5 = (f32[96,128]{1,0:T(8,128)S(1)}, f32[96,128]{1,0:T(8,128)S(1)}, u32[]{:S(2)}, u32[]{:S(2)}) collective-permute-start(f32[96,128]{1,0:T(8,128)S(1)} %join_model.1.refs_0_), channel_id=1, source_target_pairs={{0,2},{1,3},{2,0},{3,1},{4,6},{5,7},{6,4},{7,5},{8,10},{9,11},{10,... | collective-permute-start | bytes 147464 | tf_op jit(solution)/shard_map/ppermute | solution.py:516
  14.1 5.1 %collective-permute-start.4 = (f32[96,128]{1,0:T(8,128)S(1)}, f32[96,128]{1,0:T(8,128)S(1)}, u32[]{:S(2)}, u32[]{:S(2)}) collective-permute-start(f32[96,128]{1,0:T(8,128)S(1)} %join_model.1.refs_0_), channel_id=1, source_target_pairs={{0,1},{1,0},{2,3},{3,2},{4,5},{5,4},{6,7},{7,6},{8,9},{9,8},{10,11... | collective-permute-start | bytes 147464 | tf_op jit(solution)/shard_map/ppermute | solution.py:516
  21.2 5.3 %collective-permute-start.7 = (f32[48,128]{1,0:T(8,128)S(1)}, f32[48,128]{1,0:T(8,128)S(1)}, u32[]{:S(2)}, u32[]{:S(2)}) collective-permute-start(f32[48,128]{1,0:T(8,128)S(1)} %get-tuple-element.45), channel_id=1, source_target_pairs={{0,1},{1,0},{2,3},{3,2},{4,5},{5,4},{6,7},{7,6},{8,9},{9,8},{10,11... | collective-permute-start | bytes 73736 | tf_op jit(solution)/shard_map/ppermute | solution.py:516
  22.3 4.7 %collective-permute-start.8 = (f32[48,128]{1,0:T(8,128)S(1)}, f32[48,128]{1,0:T(8,128)S(1)}, u32[]{:S(2)}, u32[]{:S(2)}) collective-permute-start(f32[48,128]{1,0:T(8,128)S(1)} %get-tuple-element.46), channel_id=1, source_target_pairs={{0,2},{1,3},{2,0},{3,1},{4,6},{5,7},{6,4},{7,5},{8,10},{9,11},{10,... | collective-permute-start | bytes 73736 | tf_op jit(solution)/shard_map/ppermute | solution.py:516
  24.1 5.6 %collective-permute-start.9 = (f32[48,128]{1,0:T(8,128)S(1)}, f32[48,128]{1,0:T(8,128)S(1)}, u32[]{:S(2)}, u32[]{:S(2)}) collective-permute-start(f32[48,128]{1,0:T(8,128)S(1)} %get-tuple-element.47), channel_id=1, source_target_pairs={{0,3},{1,2},{2,1},{3,0},{4,7},{5,6},{6,5},{7,4},{8,11},{9,10},{10,... | collective-permute-start | bytes 73736 | tf_op jit(solution)/shard_map/ppermute | solution.py:516

commit v3 on v2

--- a/solution.py
+++ b/solution.py
@@ -44,36 +44,33 @@
     return lax.axis_index("depth") % 2 == 0
 
 
-def pack_model(model_ref, own_ref, first_ref, second_ref, *, reach):
+def pack(
+    model_ref,
+    current_ref,
+    previous_ref,
+    forward_ref,
+    own_ref,
+    model_first,
+    model_second,
+    field_first,
+    field_second,
+    block,
+    weights,
+    sems,
+    *,
+    steps,
+    reach,
+):
     channels, coarse_len, share, coarse_columns = model_ref.shape
     half = channels // 2
-    for z in range(coarse_len):
-        for k in range(half):
-            at = (z * half + k) * share
-            own_ref[at : at + share, 0:coarse_columns] = model_ref[k, z]
-            own_ref[at : at + share, coarse_columns:] = model_ref[k + half, z]
+    depth_len = current_ref.shape[1]
+    up, down = steps + 1, steps
     part = reach * half * share
     total = coarse_len * half * share
-    even = even_depth()
-
-    @pl.when(even)
-    def _():
-        first_ref[...] = own_ref[total - part : total, :]
-        second_ref[...] = own_ref[0:part, :]
-
-    @pl.when(jnp.logical_not(even))
-    def _():
-        first_ref[...] = own_ref[0:part, :]
-        second_ref[...] = own_ref[total - part : total, :]
-
-
-def pack_fields(
-    current_ref, previous_ref, forward_ref, field_first, field_second, weights, sems, *, steps
-):
-    depth_len = current_ref.shape[1]
-    up, down = steps + 1, steps
-
-    def fill(bottom, top):
+    model_copy = pltpu.make_async_copy(model_ref, block, sems.at[5])
+    model_copy.start()
+
+    def fill(bottom, top, model_bottom, model_top):
         copies = [
             pltpu.make_async_copy(forward_ref.at[:, 0, depth_len - 1], weights, sems.at[0]),
             pltpu.make_async_copy(
@@ -91,6 +88,14 @@
         ]
         for copy in copies:
             copy.start()
+        model_copy.wait()
+        for z in range(coarse_len):
+            for k in range(half):
+                at = (z * half + k) * share
+                own_ref[at : at + share, 0:coarse_columns] = block[k, z]
+                own_ref[at : at + share, coarse_columns:] = block[k + half, z]
+        model_bottom[...] = own_ref[total - part : total, :]
+        model_top[...] = own_ref[0:part, :]
         copies[0].wait()
         for i in range(steps):
             bottom[2 * up - 1 + i] = weights[i].astype(jnp.float32)
@@ -101,11 +106,11 @@
 
     @pl.when(even)
     def _():
-        fill(field_first, field_second)
+        fill(field_first, field_second, model_first, model_second)
 
     @pl.when(jnp.logical_not(even))
     def _():
-        fill(field_second, field_first)
+        fill(field_second, field_first, model_second, model_first)
 
 
 def join_model(own_ref, first_ref, second_ref, out_ref, *, layer, depth_count):
@@ -131,10 +136,10 @@
 
 
 def injection(
-    assign_ref,
-    source_ref,
-    residual_ref,
-    receiver_ref,
+    assign_hbm,
+    source_hbm,
+    residual_hbm,
+    receiver_hbm,
     current_ref,
     previous_ref,
     forward_ref,
@@ -143,6 +148,10 @@
     current_out,
     previous_out,
     forward_out,
+    assign_ref,
+    source_ref,
+    residual_ref,
+    receiver_ref,
     sems,
     *,
     steps,
@@ -154,6 +163,10 @@
         pltpu.make_async_copy(source, target, sems.at[n])
         for n, (source, target) in enumerate(
             [
+                (assign_hbm, assign_ref),
+                (source_hbm, source_ref),
+                (receiver_hbm, receiver_ref),
+                (residual_hbm, residual_ref),
                 (current_ref, current_out),
                 (previous_ref, previous_out),
                 (forward_ref, forward_out),
@@ -162,6 +175,8 @@
     ]
     for load in loads:
         load.start()
+    for load in loads[:4]:
+        load.wait()
     receivers = receiver_ref.shape[2]
     columns = out_ref.shape[3]
     count = out_ref.shape[1]
@@ -203,7 +218,7 @@
         else:
             scale = 1.0 if e % 2 else 0.5
         keep_ref[e] = jnp.where(close, away, 1.0) * scale
-    for load in loads:
+    for load in loads[4:]:
         load.wait()
 
 
@@ -519,28 +534,22 @@
     part = reach * half * share
     own_rows = coarse_len * half * share
     halo = 3 * steps + 1
-    own, model_first, model_second = pl.pallas_call(
-        functools.partial(pack_model, reach=reach),
-        in_specs=[VMEM],
-        out_specs=[VMEM] * 3,
-        out_shape=[local(own_rows, columns), local(part, columns), local(part, columns)],
-        name="pack_model",
+    own, model_first, model_second, field_first, field_second = pl.pallas_call(
+        functools.partial(pack, steps=steps, reach=reach),
+        in_specs=[HBM] * 4,
+        out_specs=[VMEM] * 5,
+        out_shape=[local(own_rows, columns), local(part, columns), local(part, columns)]
+        + [local(halo, rows, columns)] * 2,
+        scratch_shapes=[
+            local(*model.shape),
+            pltpu.VMEM((steps, rows, columns), jnp.bfloat16),
+            pltpu.SemaphoreType.DMA((6,)),
+        ],
+        name="pack",
         compiler_params=LIMIT,
-    )(far(model))
+    )(far(model), far(adjoint_last), far(adjoint_late), far(forward))
     model_second = moved(model_second, "depth", second_pairs)
     model_first = moved(model_first, "depth", first_pairs)
-    field_first, field_second = pl.pallas_call(
-        functools.partial(pack_fields, steps=steps),
-        in_specs=[HBM] * 3,
-        out_specs=[VMEM] * 2,
-        out_shape=[local(halo, rows, columns)] * 2,
-        scratch_shapes=[
-            pltpu.VMEM((steps, rows, columns), jnp.bfloat16),
-            pltpu.SemaphoreType.DMA((5,)),
-        ],
-        name="pack_fields",
-        compiler_params=LIMIT,
-    )(far(adjoint_last), far(adjoint_late), far(forward))
     field_second = moved(field_second, "depth", second_pairs)
     field_first = moved(field_first, "depth", first_pairs)
     height = depth_len + 2 * steps + 1
@@ -548,7 +557,7 @@
         functools.partial(
             injection, steps=steps, depth_len=depth_len, rows=rows, depth_count=depth_count
         ),
-        in_specs=[SMEM, SMEM, VMEM, VMEM, HBM, HBM, HBM],
+        in_specs=[HBM] * 7,
         out_specs=[VMEM] * 5,
         out_shape=[
             local(steps, height - 2, rows, columns),
@@ -557,7 +566,13 @@
             local(1, depth_len, rows, columns),
             pltpu.VMEM(forward.shape, forward.dtype),
         ],
-        scratch_shapes=[pltpu.SemaphoreType.DMA((3,))],
+        scratch_shapes=[
+            pltpu.SMEM(assignment.shape, jnp.int32),
+            pltpu.SMEM(source_cells.shape, jnp.int32),
+            local(*residuals.shape),
+            pltpu.VMEM((receiver_cells.shape[2],) + receiver_cells.shape[:2], jnp.int32),
+            pltpu.SemaphoreType.DMA((7,)),
+        ],
         name="injection",
         compiler_params=LIMIT,
     )(

time: 30.7 us -> 30.6 us (level)
  Pallas kernels: 7.69 us -> 6.67 us
  waiting for transfers between devices: 9.9 us -> 10.9 us
    ppermute x10, waiting for transfers between devices: 9.9 us -> 10.9 us  [moved(): return near(lax.ppermute(array, axis, pairs))]
    pallas_call x2 -> x1, Pallas kernels: 1.88 us -> 1.02 us  [local_part(): pl.pallas_call(functools.partial(pack, steps=steps, reach=reach), in_spec...]
  transfers between devices with their start and end apart: 10 -> 10, of which waited for: 5 -> 5; matrix products, arithmetic and copies ran while one was open for 0% -> 0% of each run, Pallas kernels for 13% -> 10%
where the time goes in v3:
time: 30.6 us; the launch traced here: 30.4 us
  starting transfers between devices  12.1 us (40%)
  waiting for transfers between devices  10.9 us (36%)
  Pallas kernels  6.67 us (22%)
  between operations  0.69 us (2%)
    ppermute x10, starting transfers between devices, moved(): return near(lax.ppermute(array, axis, pairs))  12.1 us
    ppermute x10, waiting for transfers between devices, moved(): return near(lax.ppermute(array, axis, pairs))  10.9 us
    pallas_call x1, Pallas kernels, local_part(): pl.pallas_call(functools.partial(march, steps=steps, shots=shots, depth_c...  1.94 us
    pallas_call x1, Pallas kernels, local_part(): pl.pallas_call(functools.partial(injection, steps=steps, depth_len=depth_...  1.72 us
    pallas_call x1, Pallas kernels, local_part(): pl.pallas_call(functools.partial(pack, steps=steps, reach=reach), in_spec...  1.02 us
    pallas_call x1, Pallas kernels, local_part(): pl.pallas_call(functools.partial(last_update, steps=steps, reach=reach),...  0.87 us
    pallas_call x1, Pallas kernels, local_part(): pl.pallas_call(functools.partial(finish, steps=steps), in_specs=[VMEM] *...  0.7 us
  transfers between devices with their start and end apart: 10, of which 5 were waited for; matrix products, arithmetic and copies ran while one was open for 0% of the time, Pallas kernels for 10%

profile of v3, /device:TPU:0, one launch (start us, length us, event | category | flops | bytes accessed | tf_op | source)
XLA Modules:
  0.0 30.4 jit_solution(17296816542418671933)
XLA Ops:
  0.6 1.0 %pack.1 = (f32[48,128]{1,0:T(8,128)S(1)}, f32[24,128]{1,0:T(8,128)S(1)}, f32[24,128]{1,0:T(8,128)S(1)}, f32[13,32,128]{2,1,0:T(8,128)S(1)}, f32[13,32,128]{2,1,0:T(8,128)S(1)}) custom-call(f32[6,4,4,64]{3,2,1,0:T(4,128)} %model_ref.1, f32[1,8,32,128]{3,2,1,0:T(8,128)} %current_ref.3, f32[1,8,32,128]{3,2,1,0:T(8,128)} %previous_ref.3, ...), custom_call_target="tpu_custom_call" | custom-call | tf_op jit(solution)/shard_map/pack/pallas_call | solution.py:537
  1.7 0.6 %collective-permute-start = (f32[13,32,128]{2,1,0:T(8,128)S(1)}, f32[13,32,128]{2,1,0:T(8,128)S(1)}, u32[]{:S(2)}, u32[]{:S(2)}) collective-permute-start(f32[13,32,128]{2,1,0:T(8,128)S(1)} %get-tuple-element.28), channel_id=1, source_target_pairs={{0,4},{4,0},{8,12},{12,8},{1,5},{5,1},{9,13},{13,9},{2,6},{6,2},{1... | collective-permute-start | bytes 638984 | tf_op jit(solution)/shard_map/ppermute | solution.py:531
  2.2 2.6 %collective-permute-start.1 = (f32[13,32,128]{2,1,0:T(8,128)S(1)}, f32[13,32,128]{2,1,0:T(8,128)S(1)}, u32[]{:S(2)}, u32[]{:S(2)}) collective-permute-start(f32[13,32,128]{2,1,0:T(8,128)S(1)} %get-tuple-element.29), channel_id=1, source_target_pairs={{0,12},{4,8},{8,4},{12,0},{1,13},{5,9},{9,5},{13,1},{2,14},{6,10},... | collective-permute-start | bytes 638984 | tf_op jit(solution)/shard_map/ppermute | solution.py:531
  4.8 0.1 collective-permute-start.2
  4.9 0.1 collective-permute-start.3
  5.0 1.0 %collective-permute-done.2.first_ref = f32[24,128]{1,0:T(8,128)S(1)} collective-permute-done((f32[24,128]{1,0:T(8,128)S(1)}, f32[24,128]{1,0:T(8,128)S(1)}, u32[]{:S(2)}, u32[]{:S(2)}) %collective-permute-start.2) | collective-permute-done | bytes 12320 | tf_op jit(solution)/shard_map/ppermute | solution.py:531
  6.0 4.6 %collective-permute-done.3.second_ref = f32[24,128]{1,0:T(8,128)S(1)} collective-permute-done((f32[24,128]{1,0:T(8,128)S(1)}, f32[24,128]{1,0:T(8,128)S(1)}, u32[]{:S(2)}, u32[]{:S(2)}) %collective-permute-start.3) | collective-permute-done | bytes 12320 | tf_op jit(solution)/shard_map/ppermute | solution.py:531
  10.6 3.5 %collective-permute-start.6 = (f32[96,128]{1,0:T(8,128)S(1)}, f32[96,128]{1,0:T(8,128)S(1)}, u32[]{:S(2)}, u32[]{:S(2)}) collective-permute-start(f32[96,128]{1,0:T(8,128)S(1)} %join_model.1.refs_0_), channel_id=1, source_target_pairs={{0,3},{1,2},{2,1},{3,0},{4,7},{5,6},{6,5},{7,4},{8,11},{9,10},{10,... | collective-permute-start | bytes 147464 | tf_op jit(solution)/shard_map/ppermute | solution.py:531
  14.1 0.0 collective-permute-start.5
  14.1 0.9 %collective-permute-start.4 = (f32[96,128]{1,0:T(8,128)S(1)}, f32[96,128]{1,0:T(8,128)S(1)}, u32[]{:S(2)}, u32[]{:S(2)}) collective-permute-start(f32[96,128]{1,0:T(8,128)S(1)} %join_model.1.refs_0_), channel_id=1, source_target_pairs={{0,1},{1,0},{2,3},{3,2},{4,5},{5,4},{6,7},{7,6},{8,9},{9,8},{10,11... | collective-permute-start | bytes 147464 | tf_op jit(solution)/shard_map/ppermute | solution.py:531
  15.0 1.7 %injection.1 = (f32[4,15,32,128]{3,2,1,0:T(8,128)S(1)}, f32[9,32,128]{2,1,0:T(8,128)S(1)}, f32[1,8,32,128]{3,2,1,0:T(8,128)S(1)}, f32[1,8,32,128]{3,2,1,0:T(8,128)S(1)}, bf16[4,1,8,32,128]{4,3,2,1,0:T(8,128)(2,1)S(1)}) custom-call(s32[4]{0:T(128)} %assign_hbm.1, s32[4,3]{1,0:T(4,128)} %source_hbm.1, f32[1,4,256]{2,1,0:T(4,128)} %residual_hbm.1, ...), custom_call_target="tpu_custom_call" | custom-call | tf_op jit(solution)/shard_map/injection/pallas_call | solution.py:556
  16.7 0.0 collective-permute-done.first_ref
  16.7 0.0 collective-permute-done.1.second_ref
  16.8 0.4 %prepare.1 = (f32[17,48,128]{2,1,0:T(8,128)S(1)}, f32[6,15,32,128]{3,2,1,0:T(8,128)S(1)}, f32[15,32,128]{2,1,0:T(8,128)S(1)}, f32[6,9,32,128]{3,2,1,0:T(8,128)S(1)}, f32[4,9,32,128]{3,2,1,0:T(8,128)S(1)}) custom-call(f32[1,8,32,128]{3,2,1,0:T(8,128)S(1)} %get-tuple-element.25.current_ref, f32[1,8,32,128]{3,2,1,0:T(8,128)S(1)} %get-tuple-element.26.previous_ref, ...), custom_call_target="tpu_custom_call" | custom-call | tf_op jit(solution)/shard_map/prepare/pallas_call | solution.py:599
  17.2 0.0 collective-permute-done.6.refs_3_
  17.2 2.0 %collective-permute-done.5.refs_2_ = f32[96,128]{1,0:T(8,128)S(1)} collective-permute-done((f32[96,128]{1,0:T(8,128)S(1)}, f32[96,128]{1,0:T(8,128)S(1)}, u32[]{:S(2)}, u32[]{:S(2)}) %collective-permute-start.5) | collective-permute-done | bytes 49184 | tf_op jit(solution)/shard_map/ppermute | solution.py:531
  19.2 0.0 collective-permute-done.4.refs_1_
  19.2 1.9 %march.1 = (f32[48,128]{1,0:T(8,128)S(1)}, f32[48,128]{1,0:T(8,128)S(1)}, f32[48,128]{1,0:T(8,128)S(1)}, f32[48,128]{1,0:T(8,128)S(1)}, f32[17,48,128]{2,1,0:T(8...) custom-call(f32[17,48,128]{2,1,0:T(8,128)S(1)} %get-tuple-element.32.field, ...), custom_call_target="tpu_custom_call" | custom-call | tf_op jit(solution)/shard_map/march/pallas_call | solution.py:634
  21.2 1.2 %collective-permute-start.7 = (f32[48,128]{1,0:T(8,128)S(1)}, f32[48,128]{1,0:T(8,128)S(1)}, u32[]{:S(2)}, u32[]{:S(2)}) collective-permute-start(f32[48,128]{1,0:T(8,128)S(1)} %get-tuple-element.45), channel_id=1, source_target_pairs={{0,1},{1,0},{2,3},{3,2},{4,5},{5,4},{6,7},{7,6},{8,9},{9,8},{10,11... | collective-permute-start | bytes 73736 | tf_op jit(solution)/shard_map/ppermute | solution.py:531
  22.3 1.8 %collective-permute-start.8 = (f32[48,128]{1,0:T(8,128)S(1)}, f32[48,128]{1,0:T(8,128)S(1)}, u32[]{:S(2)}, u32[]{:S(2)}) collective-permute-start(f32[48,128]{1,0:T(8,128)S(1)} %get-tuple-element.46), channel_id=1, source_target_pairs={{0,2},{1,3},{2,0},{3,1},{4,6},{5,7},{6,4},{7,5},{8,10},{9,11},{10,... | collective-permute-start | bytes 73736 | tf_op jit(solution)/shard_map/ppermute | solution.py:531
  24.1 1.5 %collective-permute-start.9 = (f32[48,128]{1,0:T(8,128)S(1)}, f32[48,128]{1,0:T(8,128)S(1)}, u32[]{:S(2)}, u32[]{:S(2)}) collective-permute-start(f32[48,128]{1,0:T(8,128)S(1)} %get-tuple-element.47), channel_id=1, source_target_pairs={{0,3},{1,2},{2,1},{3,0},{4,7},{5,6},{6,5},{7,4},{8,11},{9,10},{10,... | collective-permute-start | bytes 73736 | tf_op jit(solution)/shard_map/ppermute | solution.py:531
  25.6 0.9 %last_update.1 = f32[1,8,32,128]{3,2,1,0:T(8,128)} custom-call(f32[17,48,128]{2,1,0:T(8,128)S(1)} %get-tuple-element.40.refs_0_, f32[17,48,128]{2,1,0:T(8,128)S(1)} %get-tuple-element.41.refs_1_, f32[8,6,32,128]{3,2,1,0:T(8,128)S(1)} %get-tuple-element.42.refs_2_, f32[7,6,32,128]{3,2,1,0:T(8,128)S(1)} %get-tuple-element.43.refs_3_, ...), custom_call_target="tpu_custom_call" | custom-call | tf_op jit(solution)/shard_map/last_update/pallas_call | solution.py:657
  26.5 0.0 collective-permute-done.7.refs_1_
  26.5 0.6 %collective-permute-done.8.refs_2_ = f32[48,128]{1,0:T(8,128)S(1)} collective-permute-done((f32[48,128]{1,0:T(8,128)S(1)}, f32[48,128]{1,0:T(8,128)S(1)}, u32[]{:S(2)}, u32[]{:S(2)}) %collective-permute-start.8) | collective-permute-done | bytes 24608 | tf_op jit(solution)/shard_map/ppermute | solution.py:531
  27.1 2.7 %collective-permute-done.9.refs_3_ = f32[48,128]{1,0:T(8,128)S(1)} collective-permute-done((f32[48,128]{1,0:T(8,128)S(1)}, f32[48,128]{1,0:T(8,128)S(1)}, u32[]{:S(2)}, u32[]{:S(2)}) %collective-permute-start.9) | collective-permute-done | bytes 24608 | tf_op jit(solution)/shard_map/ppermute | solution.py:531
  29.8 0.7 %finish.1 = f32[6,4,4,64]{3,2,1,0:T(4,128)} custom-call(f32[48,128]{1,0:T(8,128)S(1)} %get-tuple-element.44.refs_0_, f32[48,128]{1,0:T(8,128)S(1)} %collective-permute-done.7.refs_1_, f32[48,128]{1,0:T(8,128)S(1)} %collective-permute-done.8.refs_2_, f32[48,128]{1,0:T(8,128)S(1)} %collective-permute-done.9.refs_3_), custom_call_target="tpu_custom_call" | custom-call | tf_op jit(solution)/shard_map/finish/pallas_call | solution.py:667
  (1 shorter events, 0.0 us)
Async XLA Ops:
  1.7 15.1 %collective-permute-start = (f32[13,32,128]{2,1,0:T(8,128)S(1)}, f32[13,32,128]{2,1,0:T(8,128)S(1)}, u32[]{:S(2)}, u32[]{:S(2)}) collective-permute-start(f32[13,32,128]{2,1,0:T(8,128)S(1)} %get-tuple-element.28), channel_id=1, source_target_pairs={{0,4},{4,0},{8,12},{12,8},{1,5},{5,1},{9,13},{13,9},{2,6},{6,2},{1... | collective-permute-start | bytes 638984 | tf_op jit(solution)/shard_map/ppermute | solution.py:531
  2.2 14.5 %collective-permute-start.1 = (f32[13,32,128]{2,1,0:T(8,128)S(1)}, f32[13,32,128]{2,1,0:T(8,128)S(1)}, u32[]{:S(2)}, u32[]{:S(2)}) collective-permute-start(f32[13,32,128]{2,1,0:T(8,128)S(1)} %get-tuple-element.29), channel_id=1, source_target_pairs={{0,12},{4,8},{8,4},{12,0},{1,13},{5,9},{9,5},{13,1},{2,14},{6,10},... | collective-permute-start | bytes 638984 | tf_op jit(solution)/shard_map/ppermute | solution.py:531
  4.8 1.2 %collective-permute-start.2 = (f32[24,128]{1,0:T(8,128)S(1)}, f32[24,128]{1,0:T(8,128)S(1)}, u32[]{:S(2)}, u32[]{:S(2)}) collective-permute-start(f32[24,128]{1,0:T(8,128)S(1)} %get-tuple-element.38), channel_id=1, source_target_pairs={{0,4},{4,0},{8,12},{12,8},{1,5},{5,1},{9,13},{13,9},{2,6},{6,2},{1... | collective-permute-start | bytes 36872 | tf_op jit(solution)/shard_map/ppermute | solution.py:531
  4.9 5.7 %collective-permute-start.3 = (f32[24,128]{1,0:T(8,128)S(1)}, f32[24,128]{1,0:T(8,128)S(1)}, u32[]{:S(2)}, u32[]{:S(2)}) collective-permute-start(f32[24,128]{1,0:T(8,128)S(1)} %get-tuple-element.39), channel_id=1, source_target_pairs={{0,12},{4,8},{8,4},{12,0},{1,13},{5,9},{9,5},{13,1},{2,14},{6,10},... | collective-permute-start | bytes 36872 | tf_op jit(solution)/shard_map/ppermute | solution.py:531
  10.6 6.6 %collective-permute-start.6 = (f32[96,128]{1,0:T(8,128)S(1)}, f32[96,128]{1,0:T(8,128)S(1)}, u32[]{:S(2)}, u32[]{:S(2)}) collective-permute-start(f32[96,128]{1,0:T(8,128)S(1)} %join_model.1.refs_0_), channel_id=1, source_target_pairs={{0,3},{1,2},{2,1},{3,0},{4,7},{5,6},{6,5},{7,4},{8,11},{9,10},{10,... | collective-permute-start | bytes 147464 | tf_op jit(solution)/shard_map/ppermute | solution.py:531
  14.1 5.1 %collective-permute-start.5 = (f32[96,128]{1,0:T(8,128)S(1)}, f32[96,128]{1,0:T(8,128)S(1)}, u32[]{:S(2)}, u32[]{:S(2)}) collective-permute-start(f32[96,128]{1,0:T(8,128)S(1)} %join_model.1.refs_0_), channel_id=1, source_target_pairs={{0,2},{1,3},{2,0},{3,1},{4,6},{5,7},{6,4},{7,5},{8,10},{9,11},{10,... | collective-permute-start | bytes 147464 | tf_op jit(solution)/shard_map/ppermute | solution.py:531
  14.1 5.1 %collective-permute-start.4 = (f32[96,128]{1,0:T(8,128)S(1)}, f32[96,128]{1,0:T(8,128)S(1)}, u32[]{:S(2)}, u32[]{:S(2)}) collective-permute-start(f32[96,128]{1,0:T(8,128)S(1)} %join_model.1.refs_0_), channel_id=1, source_target_pairs={{0,1},{1,0},{2,3},{3,2},{4,5},{5,4},{6,7},{7,6},{8,9},{9,8},{10,11... | collective-permute-start | bytes 147464 | tf_op jit(solution)/shard_map/ppermute | solution.py:531
  21.2 5.3 %collective-permute-start.7 = (f32[48,128]{1,0:T(8,128)S(1)}, f32[48,128]{1,0:T(8,128)S(1)}, u32[]{:S(2)}, u32[]{:S(2)}) collective-permute-start(f32[48,128]{1,0:T(8,128)S(1)} %get-tuple-element.45), channel_id=1, source_target_pairs={{0,1},{1,0},{2,3},{3,2},{4,5},{5,4},{6,7},{7,6},{8,9},{9,8},{10,11... | collective-permute-start | bytes 73736 | tf_op jit(solution)/shard_map/ppermute | solution.py:531
  22.3 4.7 %collective-permute-start.8 = (f32[48,128]{1,0:T(8,128)S(1)}, f32[48,128]{1,0:T(8,128)S(1)}, u32[]{:S(2)}, u32[]{:S(2)}) collective-permute-start(f32[48,128]{1,0:T(8,128)S(1)} %get-tuple-element.46), channel_id=1, source_target_pairs={{0,2},{1,3},{2,0},{3,1},{4,6},{5,7},{6,4},{7,5},{8,10},{9,11},{10,... | collective-permute-start | bytes 73736 | tf_op jit(solution)/shard_map/ppermute | solution.py:531
  24.1 5.6 %collective-permute-start.9 = (f32[48,128]{1,0:T(8,128)S(1)}, f32[48,128]{1,0:T(8,128)S(1)}, u32[]{:S(2)}, u32[]{:S(2)}) collective-permute-start(f32[48,128]{1,0:T(8,128)S(1)} %get-tuple-element.47), channel_id=1, source_target_pairs={{0,3},{1,2},{2,1},{3,0},{4,7},{5,6},{6,5},{7,4},{8,11},{9,10},{10,... | collective-permute-start | bytes 73736 | tf_op jit(solution)/shard_map/ppermute | solution.py:531

commit v4 on v3

--- a/solution.py
+++ b/solution.py
@@ -38,6 +38,21 @@
         stacked = jnp.concatenate([right, right], axis=0)
         return product(jnp.concatenate(parts[:2], axis=1), stacked) + product(parts[2], right)
     return product(parts[0], right) + product(parts[1], right) + product(parts[2], right)
+
+
+def pair_matrix(coarse):
+    refine = refine_matrix(coarse)
+    none = jnp.zeros_like(refine)
+    return jnp.concatenate(
+        [jnp.concatenate([refine, none], axis=1), jnp.concatenate([none, refine], axis=1)], axis=0
+    )
+
+
+def refine_early(*refs):
+    blocks, out_ref = refs[:-1], refs[-1]
+    matrix = pair_matrix(blocks[0].shape[1] // 2)
+    for j, block in enumerate(blocks):
+        out_ref[j] = exact_dot(block[...], matrix)
 
 
 def even_depth():
@@ -378,9 +393,11 @@
     depth_count,
     reach,
 ):
-    gathered, chunks = refs[:shots], refs[shots : 2 * shots]
+    early_ref, *refs = refs
+    late, refs = refs[:2], refs[2:]
+    chunks = refs[:shots]
     ones, twos, even_rows, odd_rows, blocks, packed, coarse, *lines, totals, result = refs[
-        2 * shots :
+        shots:
     ]
     across = lines[0]
     rows, columns = start_base.shape[1:]
@@ -400,12 +417,15 @@
 
     half = channels // 2
     refine = refine_matrix(columns // 2)
-    none = jnp.zeros_like(refine)
-    refine_pair = jnp.concatenate(
-        [jnp.concatenate([refine, none], axis=1), jnp.concatenate([none, refine], axis=1)], axis=0
+    count = late[0].shape[0]
+    both = exact_dot(
+        jnp.concatenate([ref[...] for ref in late], axis=0), pair_matrix(columns // 2)
     )
     for j in range(shots):
-        wide = exact_dot(gathered[j][...], refine_pair)
+        if j in (1, 2):
+            wide = both[(j - 1) * count : j * count]
+        else:
+            wide = early_ref[max(j - 2, 0)]
         start = (shot_index ^ j) * share
         for z in range(layers):
             for k in range(half):
@@ -518,7 +538,7 @@
     reach = (steps + 1) // 2
     assert shots_here == 1 and depth_count % 2 == 0 and shots & (shots - 1) == 0
     assert channels == 6 and 2 * coarse_columns == columns
-    assert steps % 2 == 0 and steps > 2 and depth_len > steps and coarse_len >= reach and share * shots * 2 == rows
+    assert shots > 2 and steps % 2 == 0 and steps > 2 and depth_len > steps and coarse_len >= reach and share * shots * 2 == rows
     f32 = jnp.float32
     shape = lambda *dims: jax.ShapeDtypeStruct(dims, f32)
     local = lambda *dims: pltpu.VMEM(dims, f32)
@@ -623,6 +643,14 @@
         near(added),
         near(keep),
     )
+    early = pl.pallas_call(
+        refine_early,
+        in_specs=[VMEM] * (shots - 2),
+        out_specs=VMEM,
+        out_shape=local(shots - 2, joined_rows, 2 * columns),
+        name="refine_early",
+        compiler_params=LIMIT,
+    )(gathered[0], *gathered[3:])
     layers = coarse_len + 2 * reach
     chunk = local(half * coarse_len * share, columns)
     lines = [
@@ -633,7 +661,7 @@
     ]
     outs = pl.pallas_call(
         functools.partial(march, steps=steps, shots=shots, depth_count=depth_count, reach=reach),
-        in_specs=[VMEM] * (6 + shots),
+        in_specs=[VMEM] * 9,
         out_specs=[VMEM] * (shots + 4),
         out_shape=[chunk] * shots
         + [
@@ -652,7 +680,7 @@
         ],
         name="march",
         compiler_params=LIMIT,
-    )(*map(near, prepared), near(added), *gathered)
+    )(*map(near, prepared), near(added), near(early), *gathered[1:3])
     chunks, kept = outs[:shots], outs[shots:]
     final = pl.pallas_call(
         functools.partial(last_update, steps=steps, reach=reach),

time: 30.6 us -> 30.6 us (level)
  transfers between devices with their start and end apart: 10 -> 10, of which waited for: 5 -> 5; matrix products, arithmetic and copies ran while one was open for 0% -> 0% of each run, Pallas kernels for 10% -> 11%
where the time goes in v4:
time: 30.6 us; the launch traced here: 30.5 us
  starting transfers between devices  12.1 us (40%)
  waiting for transfers between devices  10.7 us (35%)
  Pallas kernels  6.9 us (23%)
  between operations  0.7 us (2%)
    ppermute x10, starting transfers between devices, moved(): return near(lax.ppermute(array, axis, pairs))  12.1 us
    ppermute x10, waiting for transfers between devices, moved(): return near(lax.ppermute(array, axis, pairs))  10.7 us
    pallas_call x1, Pallas kernels, local_part(): pl.pallas_call(functools.partial(march, steps=steps, shots=shots, depth_c...  1.97 us
    pallas_call x1, Pallas kernels, local_part(): pl.pallas_call(functools.partial(injection, steps=steps, depth_len=depth_...  1.72 us
    pallas_call x1, Pallas kernels, local_part(): pl.pallas_call(functools.partial(pack, steps=steps, reach=reach), in_spec...  1.02 us
    pallas_call x1, Pallas kernels, local_part(): pl.pallas_call(functools.partial(last_update, steps=steps, reach=reach),...  0.87 us
    pallas_call x1, Pallas kernels, local_part(): pl.pallas_call(functools.partial(finish, steps=steps), in_specs=[VMEM] *...  0.7 us
  transfers between devices with their start and end apart: 10, of which 5 were waited for; matrix products, arithmetic and copies ran while one was open for 0% of the time, Pallas kernels for 11%

profile of v4, /device:TPU:0, one launch (start us, length us, event | category | flops | bytes accessed | tf_op | source)
XLA Modules:
  0.0 30.5 jit_solution(4906765484943924182)
XLA Ops:
  0.6 1.0 %pack.1 = (f32[48,128]{1,0:T(8,128)S(1)}, f32[24,128]{1,0:T(8,128)S(1)}, f32[24,128]{1,0:T(8,128)S(1)}, f32[13,32,128]{2,1,0:T(8,128)S(1)}, f32[13,32,128]{2,1,0:T(8,128)S(1)}) custom-call(f32[6,4,4,64]{3,2,1,0:T(4,128)} %model_ref.1, f32[1,8,32,128]{3,2,1,0:T(8,128)} %current_ref.3, f32[1,8,32,128]{3,2,1,0:T(8,128)} %previous_ref.3, ...), custom_call_target="tpu_custom_call" | custom-call | tf_op jit(solution)/shard_map/pack/pallas_call | solution.py:557
  1.7 0.6 %collective-permute-start = (f32[13,32,128]{2,1,0:T(8,128)S(1)}, f32[13,32,128]{2,1,0:T(8,128)S(1)}, u32[]{:S(2)}, u32[]{:S(2)}) collective-permute-start(f32[13,32,128]{2,1,0:T(8,128)S(1)} %get-tuple-element.28), channel_id=1, source_target_pairs={{0,4},{4,0},{8,12},{12,8},{1,5},{5,1},{9,13},{13,9},{2,6},{6,2},{1... | collective-permute-start | bytes 638984 | tf_op jit(solution)/shard_map/ppermute | solution.py:551
  2.2 2.6 %collective-permute-start.1 = (f32[13,32,128]{2,1,0:T(8,128)S(1)}, f32[13,32,128]{2,1,0:T(8,128)S(1)}, u32[]{:S(2)}, u32[]{:S(2)}) collective-permute-start(f32[13,32,128]{2,1,0:T(8,128)S(1)} %get-tuple-element.29), channel_id=1, source_target_pairs={{0,12},{4,8},{8,4},{12,0},{1,13},{5,9},{9,5},{13,1},{2,14},{6,10},... | collective-permute-start | bytes 638984 | tf_op jit(solution)/shard_map/ppermute | solution.py:551
  4.8 0.1 collective-permute-start.2
  4.9 0.1 collective-permute-start.3
  5.0 1.0 %collective-permute-done.2.first_ref = f32[24,128]{1,0:T(8,128)S(1)} collective-permute-done((f32[24,128]{1,0:T(8,128)S(1)}, f32[24,128]{1,0:T(8,128)S(1)}, u32[]{:S(2)}, u32[]{:S(2)}) %collective-permute-start.2) | collective-permute-done | bytes 12320 | tf_op jit(solution)/shard_map/ppermute | solution.py:551
  6.0 4.6 %collective-permute-done.3.second_ref = f32[24,128]{1,0:T(8,128)S(1)} collective-permute-done((f32[24,128]{1,0:T(8,128)S(1)}, f32[24,128]{1,0:T(8,128)S(1)}, u32[]{:S(2)}, u32[]{:S(2)}) %collective-permute-start.3) | collective-permute-done | bytes 12320 | tf_op jit(solution)/shard_map/ppermute | solution.py:551
  10.6 3.5 %collective-permute-start.4 = (f32[96,128]{1,0:T(8,128)S(1)}, f32[96,128]{1,0:T(8,128)S(1)}, u32[]{:S(2)}, u32[]{:S(2)}) collective-permute-start(f32[96,128]{1,0:T(8,128)S(1)} %join_model.1.refs_0_), channel_id=1, source_target_pairs={{0,3},{1,2},{2,1},{3,0},{4,7},{5,6},{6,5},{7,4},{8,11},{9,10},{10,... | collective-permute-start | bytes 147464 | tf_op jit(solution)/shard_map/ppermute | solution.py:551
  14.1 0.0 collective-permute-start.6
  14.1 0.9 %collective-permute-start.5 = (f32[96,128]{1,0:T(8,128)S(1)}, f32[96,128]{1,0:T(8,128)S(1)}, u32[]{:S(2)}, u32[]{:S(2)}) collective-permute-start(f32[96,128]{1,0:T(8,128)S(1)} %join_model.1.refs_0_), channel_id=1, source_target_pairs={{0,1},{1,0},{2,3},{3,2},{4,5},{5,4},{6,7},{7,6},{8,9},{9,8},{10,11... | collective-permute-start | bytes 147464 | tf_op jit(solution)/shard_map/ppermute | solution.py:551
  15.0 1.7 %injection.1 = (f32[4,15,32,128]{3,2,1,0:T(8,128)S(1)}, f32[9,32,128]{2,1,0:T(8,128)S(1)}, f32[1,8,32,128]{3,2,1,0:T(8,128)S(1)}, f32[1,8,32,128]{3,2,1,0:T(8,128)S(1)}, bf16[4,1,8,32,128]{4,3,2,1,0:T(8,128)(2,1)S(1)}) custom-call(s32[4]{0:T(128)} %assign_hbm.1, s32[4,3]{1,0:T(4,128)} %source_hbm.1, f32[1,4,256]{2,1,0:T(4,128)} %residual_hbm.1, ...), custom_call_target="tpu_custom_call" | custom-call | tf_op jit(solution)/shard_map/injection/pallas_call | solution.py:576
  16.7 0.0 collective-permute-done.4.refs_1_
  16.7 0.2 refine_early.1.refs_0_
  17.0 0.0 collective-permute-done.first_ref
  17.0 0.0 collective-permute-done.1.second_ref
  17.0 0.4 %prepare.1 = (f32[17,48,128]{2,1,0:T(8,128)S(1)}, f32[6,15,32,128]{3,2,1,0:T(8,128)S(1)}, f32[15,32,128]{2,1,0:T(8,128)S(1)}, f32[6,9,32,128]{3,2,1,0:T(8,128)S(1)}, f32[4,9,32,128]{3,2,1,0:T(8,128)S(1)}) custom-call(f32[1,8,32,128]{3,2,1,0:T(8,128)S(1)} %get-tuple-element.25.current_ref, f32[1,8,32,128]{3,2,1,0:T(8,128)S(1)} %get-tuple-element.26.previous_ref, ...), custom_call_target="tpu_custom_call" | custom-call | tf_op jit(solution)/shard_map/prepare/pallas_call | solution.py:619
  17.4 1.8 %collective-permute-done.6.refs_2_ = f32[96,128]{1,0:T(8,128)S(1)} collective-permute-done((f32[96,128]{1,0:T(8,128)S(1)}, f32[96,128]{1,0:T(8,128)S(1)}, u32[]{:S(2)}, u32[]{:S(2)}) %collective-permute-start.6) | collective-permute-done | bytes 49184 | tf_op jit(solution)/shard_map/ppermute | solution.py:551
  19.2 0.0 collective-permute-done.5.refs_1_
  19.2 2.0 %march.1 = (f32[48,128]{1,0:T(8,128)S(1)}, f32[48,128]{1,0:T(8,128)S(1)}, f32[48,128]{1,0:T(8,128)S(1)}, f32[48,128]{1,0:T(8,128)S(1)}, f32[17,48,128]{2,1,0:T(8...) custom-call(f32[17,48,128]{2,1,0:T(8,128)S(1)} %get-tuple-element.32.field, ...), custom_call_target="tpu_custom_call" | custom-call | tf_op jit(solution)/shard_map/march/pallas_call | solution.py:662
  21.2 1.2 %collective-permute-start.7 = (f32[48,128]{1,0:T(8,128)S(1)}, f32[48,128]{1,0:T(8,128)S(1)}, u32[]{:S(2)}, u32[]{:S(2)}) collective-permute-start(f32[48,128]{1,0:T(8,128)S(1)} %get-tuple-element.45), channel_id=1, source_target_pairs={{0,1},{1,0},{2,3},{3,2},{4,5},{5,4},{6,7},{7,6},{8,9},{9,8},{10,11... | collective-permute-start | bytes 73736 | tf_op jit(solution)/shard_map/ppermute | solution.py:551
  22.4 1.8 %collective-permute-start.8 = (f32[48,128]{1,0:T(8,128)S(1)}, f32[48,128]{1,0:T(8,128)S(1)}, u32[]{:S(2)}, u32[]{:S(2)}) collective-permute-start(f32[48,128]{1,0:T(8,128)S(1)} %get-tuple-element.46), channel_id=1, source_target_pairs={{0,2},{1,3},{2,0},{3,1},{4,6},{5,7},{6,4},{7,5},{8,10},{9,11},{10,... | collective-permute-start | bytes 73736 | tf_op jit(solution)/shard_map/ppermute | solution.py:551
  24.1 1.5 %collective-permute-start.9 = (f32[48,128]{1,0:T(8,128)S(1)}, f32[48,128]{1,0:T(8,128)S(1)}, u32[]{:S(2)}, u32[]{:S(2)}) collective-permute-start(f32[48,128]{1,0:T(8,128)S(1)} %get-tuple-element.47), channel_id=1, source_target_pairs={{0,3},{1,2},{2,1},{3,0},{4,7},{5,6},{6,5},{7,4},{8,11},{9,10},{10,... | collective-permute-start | bytes 73736 | tf_op jit(solution)/shard_map/ppermute | solution.py:551
  25.7 0.9 %last_update.1 = f32[1,8,32,128]{3,2,1,0:T(8,128)} custom-call(f32[17,48,128]{2,1,0:T(8,128)S(1)} %get-tuple-element.40.refs_0_, f32[17,48,128]{2,1,0:T(8,128)S(1)} %get-tuple-element.41.refs_1_, f32[8,6,32,128]{3,2,1,0:T(8,128)S(1)} %get-tuple-element.42.refs_2_, f32[7,6,32,128]{3,2,1,0:T(8,128)S(1)} %get-tuple-element.43.refs_3_, ...), custom_call_target="tpu_custom_call" | custom-call | tf_op jit(solution)/shard_map/last_update/pallas_call | solution.py:685
  26.5 0.0 collective-permute-done.7.refs_1_
  26.5 0.6 %collective-permute-done.8.refs_2_ = f32[48,128]{1,0:T(8,128)S(1)} collective-permute-done((f32[48,128]{1,0:T(8,128)S(1)}, f32[48,128]{1,0:T(8,128)S(1)}, u32[]{:S(2)}, u32[]{:S(2)}) %collective-permute-start.8) | collective-permute-done | bytes 24608 | tf_op jit(solution)/shard_map/ppermute | solution.py:551
  27.1 2.7 %collective-permute-done.9.refs_3_ = f32[48,128]{1,0:T(8,128)S(1)} collective-permute-done((f32[48,128]{1,0:T(8,128)S(1)}, f32[48,128]{1,0:T(8,128)S(1)}, u32[]{:S(2)}, u32[]{:S(2)}) %collective-permute-start.9) | collective-permute-done | bytes 24608 | tf_op jit(solution)/shard_map/ppermute | solution.py:551
  29.8 0.7 %finish.1 = f32[6,4,4,64]{3,2,1,0:T(4,128)} custom-call(f32[48,128]{1,0:T(8,128)S(1)} %get-tuple-element.44.refs_0_, f32[48,128]{1,0:T(8,128)S(1)} %collective-permute-done.7.refs_1_, f32[48,128]{1,0:T(8,128)S(1)} %collective-permute-done.8.refs_2_, f32[48,128]{1,0:T(8,128)S(1)} %collective-permute-done.9.refs_3_), custom_call_target="tpu_custom_call" | custom-call | tf_op jit(solution)/shard_map/finish/pallas_call | solution.py:695
  (1 shorter events, 0.0 us)
Async XLA Ops:
  1.7 15.3 %collective-permute-start = (f32[13,32,128]{2,1,0:T(8,128)S(1)}, f32[13,32,128]{2,1,0:T(8,128)S(1)}, u32[]{:S(2)}, u32[]{:S(2)}) collective-permute-start(f32[13,32,128]{2,1,0:T(8,128)S(1)} %get-tuple-element.28), channel_id=1, source_target_pairs={{0,4},{4,0},{8,12},{12,8},{1,5},{5,1},{9,13},{13,9},{2,6},{6,2},{1... | collective-permute-start | bytes 638984 | tf_op jit(solution)/shard_map/ppermute | solution.py:551
  2.2 14.8 %collective-permute-start.1 = (f32[13,32,128]{2,1,0:T(8,128)S(1)}, f32[13,32,128]{2,1,0:T(8,128)S(1)}, u32[]{:S(2)}, u32[]{:S(2)}) collective-permute-start(f32[13,32,128]{2,1,0:T(8,128)S(1)} %get-tuple-element.29), channel_id=1, source_target_pairs={{0,12},{4,8},{8,4},{12,0},{1,13},{5,9},{9,5},{13,1},{2,14},{6,10},... | collective-permute-start | bytes 638984 | tf_op jit(solution)/shard_map/ppermute | solution.py:551
  4.8 1.2 %collective-permute-start.2 = (f32[24,128]{1,0:T(8,128)S(1)}, f32[24,128]{1,0:T(8,128)S(1)}, u32[]{:S(2)}, u32[]{:S(2)}) collective-permute-start(f32[24,128]{1,0:T(8,128)S(1)} %get-tuple-element.38), channel_id=1, source_target_pairs={{0,4},{4,0},{8,12},{12,8},{1,5},{5,1},{9,13},{13,9},{2,6},{6,2},{1... | collective-permute-start | bytes 36872 | tf_op jit(solution)/shard_map/ppermute | solution.py:551
  4.9 5.7 %collective-permute-start.3 = (f32[24,128]{1,0:T(8,128)S(1)}, f32[24,128]{1,0:T(8,128)S(1)}, u32[]{:S(2)}, u32[]{:S(2)}) collective-permute-start(f32[24,128]{1,0:T(8,128)S(1)} %get-tuple-element.39), channel_id=1, source_target_pairs={{0,12},{4,8},{8,4},{12,0},{1,13},{5,9},{9,5},{13,1},{2,14},{6,10},... | collective-permute-start | bytes 36872 | tf_op jit(solution)/shard_map/ppermute | solution.py:551
  10.6 6.1 %collective-permute-start.4 = (f32[96,128]{1,0:T(8,128)S(1)}, f32[96,128]{1,0:T(8,128)S(1)}, u32[]{:S(2)}, u32[]{:S(2)}) collective-permute-start(f32[96,128]{1,0:T(8,128)S(1)} %join_model.1.refs_0_), channel_id=1, source_target_pairs={{0,3},{1,2},{2,1},{3,0},{4,7},{5,6},{6,5},{7,4},{8,11},{9,10},{10,... | collective-permute-start | bytes 147464 | tf_op jit(solution)/shard_map/ppermute | solution.py:551
  14.1 5.1 %collective-permute-start.6 = (f32[96,128]{1,0:T(8,128)S(1)}, f32[96,128]{1,0:T(8,128)S(1)}, u32[]{:S(2)}, u32[]{:S(2)}) collective-permute-start(f32[96,128]{1,0:T(8,128)S(1)} %join_model.1.refs_0_), channel_id=1, source_target_pairs={{0,2},{1,3},{2,0},{3,1},{4,6},{5,7},{6,4},{7,5},{8,10},{9,11},{10,... | collective-permute-start | bytes 147464 | tf_op jit(solution)/shard_map/ppermute | solution.py:551
  14.1 5.1 %collective-permute-start.5 = (f32[96,128]{1,0:T(8,128)S(1)}, f32[96,128]{1,0:T(8,128)S(1)}, u32[]{:S(2)}, u32[]{:S(2)}) collective-permute-start(f32[96,128]{1,0:T(8,128)S(1)} %join_model.1.refs_0_), channel_id=1, source_target_pairs={{0,1},{1,0},{2,3},{3,2},{4,5},{5,4},{6,7},{7,6},{8,9},{9,8},{10,11... | collective-permute-start | bytes 147464 | tf_op jit(solution)/shard_map/ppermute | solution.py:551
  21.2 5.3 %collective-permute-start.7 = (f32[48,128]{1,0:T(8,128)S(1)}, f32[48,128]{1,0:T(8,128)S(1)}, u32[]{:S(2)}, u32[]{:S(2)}) collective-permute-start(f32[48,128]{1,0:T(8,128)S(1)} %get-tuple-element.45), channel_id=1, source_target_pairs={{0,1},{1,0},{2,3},{3,2},{4,5},{5,4},{6,7},{7,6},{8,9},{9,8},{10,11... | collective-permute-start | bytes 73736 | tf_op jit(solution)/shard_map/ppermute | solution.py:551
  22.4 4.7 %collective-permute-start.8 = (f32[48,128]{1,0:T(8,128)S(1)}, f32[48,128]{1,0:T(8,128)S(1)}, u32[]{:S(2)}, u32[]{:S(2)}) collective-permute-start(f32[48,128]{1,0:T(8,128)S(1)} %get-tuple-element.46), channel_id=1, source_target_pairs={{0,2},{1,3},{2,0},{3,1},{4,6},{5,7},{6,4},{7,5},{8,10},{9,11},{10,... | collective-permute-start | bytes 73736 | tf_op jit(solution)/shard_map/ppermute | solution.py:551
  24.1 5.6 %collective-permute-start.9 = (f32[48,128]{1,0:T(8,128)S(1)}, f32[48,128]{1,0:T(8,128)S(1)}, u32[]{:S(2)}, u32[]{:S(2)}) collective-permute-start(f32[48,128]{1,0:T(8,128)S(1)} %get-tuple-element.47), channel_id=1, source_target_pairs={{0,3},{1,2},{2,1},{3,0},{4,7},{5,6},{6,5},{7,4},{8,11},{9,10},{10,... | collective-permute-start | bytes 73736 | tf_op jit(solution)/shard_map/ppermute | solution.py:551

commit v5 on v4

--- a/solution.py
+++ b/solution.py
@@ -417,15 +417,9 @@
 
     half = channels // 2
     refine = refine_matrix(columns // 2)
-    count = late[0].shape[0]
-    both = exact_dot(
-        jnp.concatenate([ref[...] for ref in late], axis=0), pair_matrix(columns // 2)
-    )
+    matrix = pair_matrix(columns // 2)
     for j in range(shots):
-        if j in (1, 2):
-            wide = both[(j - 1) * count : j * count]
-        else:
-            wide = early_ref[max(j - 2, 0)]
+        wide = exact_dot(late[j - 1][...], matrix) if j in (1, 2) else early_ref[max(j - 2, 0)]
         start = (shot_index ^ j) * share
         for z in range(layers):
             for k in range(half):

time: 30.6 us -> 30.6 us (level)
  no operation moved by 1% of the time
where the time goes in v5:
time: 30.6 us; the launch traced here: 30.4 us
  starting transfers between devices  12.1 us (40%)
  waiting for transfers between devices  10.7 us (35%)
  Pallas kernels  6.83 us (22%)
  between operations  0.7 us (2%)
    ppermute x10, starting transfers between devices, moved(): return near(lax.ppermute(array, axis, pairs))  12.1 us
    ppermute x10, waiting for transfers between devices, moved(): return near(lax.ppermute(array, axis, pairs))  10.7 us
    pallas_call x1, Pallas kernels, local_part(): pl.pallas_call(functools.partial(march, steps=steps, shots=shots, depth_c...  1.9 us
    pallas_call x1, Pallas kernels, local_part(): pl.pallas_call(functools.partial(injection, steps=steps, depth_len=depth_...  1.72 us
    pallas_call x1, Pallas kernels, local_part(): pl.pallas_call(functools.partial(pack, steps=steps, reach=reach), in_spec...  1.02 us
    pallas_call x1, Pallas kernels, local_part(): pl.pallas_call(functools.partial(last_update, steps=steps, reach=reach),...  0.87 us
    pallas_call x1, Pallas kernels, local_part(): pl.pallas_call(functools.partial(finish, steps=steps), in_specs=[VMEM] *...  0.7 us
  transfers between devices with their start and end apart: 10, of which 5 were waited for; matrix products, arithmetic and copies ran while one was open for 0% of the time, Pallas kernels for 11%

profile of v5, /device:TPU:0, one launch (start us, length us, event | category | flops | bytes accessed | tf_op | source)
XLA Modules:
  0.0 30.4 jit_solution(18443707482309625904)
XLA Ops:
  0.6 1.0 %pack.1 = (f32[48,128]{1,0:T(8,128)S(1)}, f32[24,128]{1,0:T(8,128)S(1)}, f32[24,128]{1,0:T(8,128)S(1)}, f32[13,32,128]{2,1,0:T(8,128)S(1)}, f32[13,32,128]{2,1,0:T(8,128)S(1)}) custom-call(f32[6,4,4,64]{3,2,1,0:T(4,128)} %model_ref.1, f32[1,8,32,128]{3,2,1,0:T(8,128)} %current_ref.3, f32[1,8,32,128]{3,2,1,0:T(8,128)} %previous_ref.3, ...), custom_call_target="tpu_custom_call" | custom-call | tf_op jit(solution)/shard_map/pack/pallas_call | solution.py:551
  1.7 0.6 %collective-permute-start = (f32[13,32,128]{2,1,0:T(8,128)S(1)}, f32[13,32,128]{2,1,0:T(8,128)S(1)}, u32[]{:S(2)}, u32[]{:S(2)}) collective-permute-start(f32[13,32,128]{2,1,0:T(8,128)S(1)} %get-tuple-element.28), channel_id=1, source_target_pairs={{0,4},{4,0},{8,12},{12,8},{1,5},{5,1},{9,13},{13,9},{2,6},{6,2},{1... | collective-permute-start | bytes 638984 | tf_op jit(solution)/shard_map/ppermute | solution.py:545
  2.2 2.6 %collective-permute-start.1 = (f32[13,32,128]{2,1,0:T(8,128)S(1)}, f32[13,32,128]{2,1,0:T(8,128)S(1)}, u32[]{:S(2)}, u32[]{:S(2)}) collective-permute-start(f32[13,32,128]{2,1,0:T(8,128)S(1)} %get-tuple-element.29), channel_id=1, source_target_pairs={{0,12},{4,8},{8,4},{12,0},{1,13},{5,9},{9,5},{13,1},{2,14},{6,10},... | collective-permute-start | bytes 638984 | tf_op jit(solution)/shard_map/ppermute | solution.py:545
  4.8 0.1 collective-permute-start.2
  4.9 0.1 collective-permute-start.3
  5.0 1.0 %collective-permute-done.2.first_ref = f32[24,128]{1,0:T(8,128)S(1)} collective-permute-done((f32[24,128]{1,0:T(8,128)S(1)}, f32[24,128]{1,0:T(8,128)S(1)}, u32[]{:S(2)}, u32[]{:S(2)}) %collective-permute-start.2) | collective-permute-done | bytes 12320 | tf_op jit(solution)/shard_map/ppermute | solution.py:545
  6.0 4.6 %collective-permute-done.3.second_ref = f32[24,128]{1,0:T(8,128)S(1)} collective-permute-done((f32[24,128]{1,0:T(8,128)S(1)}, f32[24,128]{1,0:T(8,128)S(1)}, u32[]{:S(2)}, u32[]{:S(2)}) %collective-permute-start.3) | collective-permute-done | bytes 12320 | tf_op jit(solution)/shard_map/ppermute | solution.py:545
  10.6 3.5 %collective-permute-start.4 = (f32[96,128]{1,0:T(8,128)S(1)}, f32[96,128]{1,0:T(8,128)S(1)}, u32[]{:S(2)}, u32[]{:S(2)}) collective-permute-start(f32[96,128]{1,0:T(8,128)S(1)} %join_model.1.refs_0_), channel_id=1, source_target_pairs={{0,3},{1,2},{2,1},{3,0},{4,7},{5,6},{6,5},{7,4},{8,11},{9,10},{10,... | collective-permute-start | bytes 147464 | tf_op jit(solution)/shard_map/ppermute | solution.py:545
  14.1 0.0 collective-permute-start.6
  14.1 0.9 %collective-permute-start.5 = (f32[96,128]{1,0:T(8,128)S(1)}, f32[96,128]{1,0:T(8,128)S(1)}, u32[]{:S(2)}, u32[]{:S(2)}) collective-permute-start(f32[96,128]{1,0:T(8,128)S(1)} %join_model.1.refs_0_), channel_id=1, source_target_pairs={{0,1},{1,0},{2,3},{3,2},{4,5},{5,4},{6,7},{7,6},{8,9},{9,8},{10,11... | collective-permute-start | bytes 147464 | tf_op jit(solution)/shard_map/ppermute | solution.py:545
  15.0 1.7 %injection.1 = (f32[4,15,32,128]{3,2,1,0:T(8,128)S(1)}, f32[9,32,128]{2,1,0:T(8,128)S(1)}, f32[1,8,32,128]{3,2,1,0:T(8,128)S(1)}, f32[1,8,32,128]{3,2,1,0:T(8,128)S(1)}, bf16[4,1,8,32,128]{4,3,2,1,0:T(8,128)(2,1)S(1)}) custom-call(s32[4]{0:T(128)} %assign_hbm.1, s32[4,3]{1,0:T(4,128)} %source_hbm.1, f32[1,4,256]{2,1,0:T(4,128)} %residual_hbm.1, ...), custom_call_target="tpu_custom_call" | custom-call | tf_op jit(solution)/shard_map/injection/pallas_call | solution.py:570
  16.7 0.0 collective-permute-done.4.refs_1_
  16.7 0.2 refine_early.1.refs_0_
  17.0 0.0 collective-permute-done.first_ref
  17.0 0.0 collective-permute-done.1.second_ref
  17.0 0.4 %prepare.1 = (f32[17,48,128]{2,1,0:T(8,128)S(1)}, f32[6,15,32,128]{3,2,1,0:T(8,128)S(1)}, f32[15,32,128]{2,1,0:T(8,128)S(1)}, f32[6,9,32,128]{3,2,1,0:T(8,128)S(1)}, f32[4,9,32,128]{3,2,1,0:T(8,128)S(1)}) custom-call(f32[1,8,32,128]{3,2,1,0:T(8,128)S(1)} %get-tuple-element.25.current_ref, f32[1,8,32,128]{3,2,1,0:T(8,128)S(1)} %get-tuple-element.26.previous_ref, ...), custom_call_target="tpu_custom_call" | custom-call | tf_op jit(solution)/shard_map/prepare/pallas_call | solution.py:613
  17.4 1.8 %collective-permute-done.6.refs_2_ = f32[96,128]{1,0:T(8,128)S(1)} collective-permute-done((f32[96,128]{1,0:T(8,128)S(1)}, f32[96,128]{1,0:T(8,128)S(1)}, u32[]{:S(2)}, u32[]{:S(2)}) %collective-permute-start.6) | collective-permute-done | bytes 49184 | tf_op jit(solution)/shard_map/ppermute | solution.py:545
  19.2 0.0 collective-permute-done.5.refs_1_
  19.2 1.9 %march.1 = (f32[48,128]{1,0:T(8,128)S(1)}, f32[48,128]{1,0:T(8,128)S(1)}, f32[48,128]{1,0:T(8,128)S(1)}, f32[48,128]{1,0:T(8,128)S(1)}, f32[17,48,128]{2,1,0:T(8...) custom-call(f32[17,48,128]{2,1,0:T(8,128)S(1)} %get-tuple-element.32.field, ...), custom_call_target="tpu_custom_call" | custom-call | tf_op jit(solution)/shard_map/march/pallas_call | solution.py:656
  21.1 1.2 %collective-permute-start.7 = (f32[48,128]{1,0:T(8,128)S(1)}, f32[48,128]{1,0:T(8,128)S(1)}, u32[]{:S(2)}, u32[]{:S(2)}) collective-permute-start(f32[48,128]{1,0:T(8,128)S(1)} %get-tuple-element.45), channel_id=1, source_target_pairs={{0,1},{1,0},{2,3},{3,2},{4,5},{5,4},{6,7},{7,6},{8,9},{9,8},{10,11... | collective-permute-start | bytes 73736 | tf_op jit(solution)/shard_map/ppermute | solution.py:545
  22.3 1.8 %collective-permute-start.8 = (f32[48,128]{1,0:T(8,128)S(1)}, f32[48,128]{1,0:T(8,128)S(1)}, u32[]{:S(2)}, u32[]{:S(2)}) collective-permute-start(f32[48,128]{1,0:T(8,128)S(1)} %get-tuple-element.46), channel_id=1, source_target_pairs={{0,2},{1,3},{2,0},{3,1},{4,6},{5,7},{6,4},{7,5},{8,10},{9,11},{10,... | collective-permute-start | bytes 73736 | tf_op jit(solution)/shard_map/ppermute | solution.py:545
  24.1 1.5 %collective-permute-start.9 = (f32[48,128]{1,0:T(8,128)S(1)}, f32[48,128]{1,0:T(8,128)S(1)}, u32[]{:S(2)}, u32[]{:S(2)}) collective-permute-start(f32[48,128]{1,0:T(8,128)S(1)} %get-tuple-element.47), channel_id=1, source_target_pairs={{0,3},{1,2},{2,1},{3,0},{4,7},{5,6},{6,5},{7,4},{8,11},{9,10},{10,... | collective-permute-start | bytes 73736 | tf_op jit(solution)/shard_map/ppermute | solution.py:545
  25.6 0.9 %last_update.1 = f32[1,8,32,128]{3,2,1,0:T(8,128)} custom-call(f32[17,48,128]{2,1,0:T(8,128)S(1)} %get-tuple-element.40.refs_0_, f32[17,48,128]{2,1,0:T(8,128)S(1)} %get-tuple-element.41.refs_1_, f32[8,6,32,128]{3,2,1,0:T(8,128)S(1)} %get-tuple-element.42.refs_2_, f32[7,6,32,128]{3,2,1,0:T(8,128)S(1)} %get-tuple-element.43.refs_3_, ...), custom_call_target="tpu_custom_call" | custom-call | tf_op jit(solution)/shard_map/last_update/pallas_call | solution.py:679
  26.5 0.0 collective-permute-done.7.refs_1_
  26.5 0.6 %collective-permute-done.8.refs_2_ = f32[48,128]{1,0:T(8,128)S(1)} collective-permute-done((f32[48,128]{1,0:T(8,128)S(1)}, f32[48,128]{1,0:T(8,128)S(1)}, u32[]{:S(2)}, u32[]{:S(2)}) %collective-permute-start.8) | collective-permute-done | bytes 24608 | tf_op jit(solution)/shard_map/ppermute | solution.py:545
  27.0 2.7 %collective-permute-done.9.refs_3_ = f32[48,128]{1,0:T(8,128)S(1)} collective-permute-done((f32[48,128]{1,0:T(8,128)S(1)}, f32[48,128]{1,0:T(8,128)S(1)}, u32[]{:S(2)}, u32[]{:S(2)}) %collective-permute-start.9) | collective-permute-done | bytes 24608 | tf_op jit(solution)/shard_map/ppermute | solution.py:545
  29.7 0.7 %finish.1 = f32[6,4,4,64]{3,2,1,0:T(4,128)} custom-call(f32[48,128]{1,0:T(8,128)S(1)} %get-tuple-element.44.refs_0_, f32[48,128]{1,0:T(8,128)S(1)} %collective-permute-done.7.refs_1_, f32[48,128]{1,0:T(8,128)S(1)} %collective-permute-done.8.refs_2_, f32[48,128]{1,0:T(8,128)S(1)} %collective-permute-done.9.refs_3_), custom_call_target="tpu_custom_call" | custom-call | tf_op jit(solution)/shard_map/finish/pallas_call | solution.py:689
  (1 shorter events, 0.0 us)
Async XLA Ops:
  1.7 15.3 %collective-permute-start = (f32[13,32,128]{2,1,0:T(8,128)S(1)}, f32[13,32,128]{2,1,0:T(8,128)S(1)}, u32[]{:S(2)}, u32[]{:S(2)}) collective-permute-start(f32[13,32,128]{2,1,0:T(8,128)S(1)} %get-tuple-element.28), channel_id=1, source_target_pairs={{0,4},{4,0},{8,12},{12,8},{1,5},{5,1},{9,13},{13,9},{2,6},{6,2},{1... | collective-permute-start | bytes 638984 | tf_op jit(solution)/shard_map/ppermute | solution.py:545
  2.2 14.8 %collective-permute-start.1 = (f32[13,32,128]{2,1,0:T(8,128)S(1)}, f32[13,32,128]{2,1,0:T(8,128)S(1)}, u32[]{:S(2)}, u32[]{:S(2)}) collective-permute-start(f32[13,32,128]{2,1,0:T(8,128)S(1)} %get-tuple-element.29), channel_id=1, source_target_pairs={{0,12},{4,8},{8,4},{12,0},{1,13},{5,9},{9,5},{13,1},{2,14},{6,10},... | collective-permute-start | bytes 638984 | tf_op jit(solution)/shard_map/ppermute | solution.py:545
  4.8 1.2 %collective-permute-start.2 = (f32[24,128]{1,0:T(8,128)S(1)}, f32[24,128]{1,0:T(8,128)S(1)}, u32[]{:S(2)}, u32[]{:S(2)}) collective-permute-start(f32[24,128]{1,0:T(8,128)S(1)} %get-tuple-element.38), channel_id=1, source_target_pairs={{0,4},{4,0},{8,12},{12,8},{1,5},{5,1},{9,13},{13,9},{2,6},{6,2},{1... | collective-permute-start | bytes 36872 | tf_op jit(solution)/shard_map/ppermute | solution.py:545
  4.9 5.7 %collective-permute-start.3 = (f32[24,128]{1,0:T(8,128)S(1)}, f32[24,128]{1,0:T(8,128)S(1)}, u32[]{:S(2)}, u32[]{:S(2)}) collective-permute-start(f32[24,128]{1,0:T(8,128)S(1)} %get-tuple-element.39), channel_id=1, source_target_pairs={{0,12},{4,8},{8,4},{12,0},{1,13},{5,9},{9,5},{13,1},{2,14},{6,10},... | collective-permute-start | bytes 36872 | tf_op jit(solution)/shard_map/ppermute | solution.py:545
  10.6 6.1 %collective-permute-start.4 = (f32[96,128]{1,0:T(8,128)S(1)}, f32[96,128]{1,0:T(8,128)S(1)}, u32[]{:S(2)}, u32[]{:S(2)}) collective-permute-start(f32[96,128]{1,0:T(8,128)S(1)} %join_model.1.refs_0_), channel_id=1, source_target_pairs={{0,3},{1,2},{2,1},{3,0},{4,7},{5,6},{6,5},{7,4},{8,11},{9,10},{10,... | collective-permute-start | bytes 147464 | tf_op jit(solution)/shard_map/ppermute | solution.py:545
  14.1 5.1 %collective-permute-start.6 = (f32[96,128]{1,0:T(8,128)S(1)}, f32[96,128]{1,0:T(8,128)S(1)}, u32[]{:S(2)}, u32[]{:S(2)}) collective-permute-start(f32[96,128]{1,0:T(8,128)S(1)} %join_model.1.refs_0_), channel_id=1, source_target_pairs={{0,2},{1,3},{2,0},{3,1},{4,6},{5,7},{6,4},{7,5},{8,10},{9,11},{10,... | collective-permute-start | bytes 147464 | tf_op jit(solution)/shard_map/ppermute | solution.py:545
  14.1 5.1 %collective-permute-start.5 = (f32[96,128]{1,0:T(8,128)S(1)}, f32[96,128]{1,0:T(8,128)S(1)}, u32[]{:S(2)}, u32[]{:S(2)}) collective-permute-start(f32[96,128]{1,0:T(8,128)S(1)} %join_model.1.refs_0_), channel_id=1, source_target_pairs={{0,1},{1,0},{2,3},{3,2},{4,5},{5,4},{6,7},{7,6},{8,9},{9,8},{10,11... | collective-permute-start | bytes 147464 | tf_op jit(solution)/shard_map/ppermute | solution.py:545
  21.1 5.3 %collective-permute-start.7 = (f32[48,128]{1,0:T(8,128)S(1)}, f32[48,128]{1,0:T(8,128)S(1)}, u32[]{:S(2)}, u32[]{:S(2)}) collective-permute-start(f32[48,128]{1,0:T(8,128)S(1)} %get-tuple-element.45), channel_id=1, source_target_pairs={{0,1},{1,0},{2,3},{3,2},{4,5},{5,4},{6,7},{7,6},{8,9},{9,8},{10,11... | collective-permute-start | bytes 73736 | tf_op jit(solution)/shard_map/ppermute | solution.py:545
  22.3 4.7 %collective-permute-start.8 = (f32[48,128]{1,0:T(8,128)S(1)}, f32[48,128]{1,0:T(8,128)S(1)}, u32[]{:S(2)}, u32[]{:S(2)}) collective-permute-start(f32[48,128]{1,0:T(8,128)S(1)} %get-tuple-element.46), channel_id=1, source_target_pairs={{0,2},{1,3},{2,0},{3,1},{4,6},{5,7},{6,4},{7,5},{8,10},{9,11},{10,... | collective-permute-start | bytes 73736 | tf_op jit(solution)/shard_map/ppermute | solution.py:545
  24.1 5.6 %collective-permute-start.9 = (f32[48,128]{1,0:T(8,128)S(1)}, f32[48,128]{1,0:T(8,128)S(1)}, u32[]{:S(2)}, u32[]{:S(2)}) collective-permute-start(f32[48,128]{1,0:T(8,128)S(1)} %get-tuple-element.47), channel_id=1, source_target_pairs={{0,3},{1,2},{2,1},{3,0},{4,7},{5,6},{6,5},{7,4},{8,11},{9,10},{10,... | collective-permute-start | bytes 73736 | tf_op jit(solution)/shard_map/ppermute | solution.py:545
